TPU v7x, 128 devices: a whole 4x4x4 slice. The times are simulated.
128 devices in a mesh: member: 8 (over x, core), region: 16 (over z, y).
Axes of the slice: x: 4, y: 4, z: 4, core: 2. Of those that a mesh axis runs over, the one named last changes fastest.
Arguments:
- ensemble: float32 [24, 32, 128, 512], P('member', 'region'), may hold values from -6 to 6
- obs_value: float32 [32, 128, 128], P(None, ('member', 'region')), may hold values from -6 to 6
- obs_error: float32 [32, 128, 128], P(None, ('member', 'region')), may hold values from 0.5 to 4
- obs_index: int32 [32, 128, 128], P(None, ('member', 'region')), may hold values from 0 to 511
- obs_count: int32 [32, 128], P(None, ('member', 'region')), may hold values from 1 to 128
Outputs:
- analysis: float32 [24, 32, 128, 512], P('member', 'region')
Inputs may be any that keep to these rules, and one draw needn't show every extreme that they name: `obs_index`: value v names field v // (256) (0 SST, 1 SSH) at cell v mod (256) of the block, cells row-major. `obs_count`: slots below a block's count are observations; the others are padding and carry no weight.
All inputs are finite; a program needn't handle non-finite values.
Results may differ from a plain program's by a relative error of at most 0.0001.
Values sent between devices are 32-bit elements; how exact they have to be, the bound alone decides.
No kernel may reach another device: no remote copies, remote signals or barrier semaphores. Data moves between devices by JAX's collectives and lax.ppermute only.
A program may use at most 64 MiB of HBM per device.

v0:
```python
import math

import jax
import jax.numpy as jnp
from jax import lax
from jax.experimental import pallas as pl
from jax.experimental.pallas import tpu as pltpu
from jax.sharding import PartitionSpec as P


SIDE = 16
NS_ITERS = 6
MEMBERS = 24
OBS = 128
VALS = 512
INFLATION_FACTOR = 1.1
INV_SCALE = 1.0 / 288.0

GROUPS = 8
HELD = MEMBERS // GROUPS
ROWS = 2
COLS = 16
BLOCKS = ROWS * COLS
POINTS = 4
EXT_COLS = COLS + 2
FIELD_ROWS = BLOCKS * 4
PITCH = FIELD_ROWS + 4
SLAB = 26
WIDE = 32
SLAB_ROWS = 472
EDGE_PITCH = 20
MAT = MEMBERS + 4
BLOCK_MAT = POINTS * MAT


def first_row(i, c):
    return i * 64 + (c >> 3) * 32 + (c & 7)


def split_bf16(x):
    high = x.astype(jnp.bfloat16)
    low = (x - high.astype(jnp.float32)).astype(jnp.bfloat16)
    return high, low


def observe_kernel(m_ref, *refs):
    parts = refs[:GROUPS]
    obs_ref, west_ref, east_ref, ens_ref, slab0_ref, slab1_ref, edge = refs[GROUPS:]
    slabs = (slab0_ref, slab1_ref)
    m = m_ref[0]
    for s in range(GROUPS):
        for k in range(HELD):
            member = (m ^ s) * HELD + k
            ens_ref[pl.ds(member * PITCH, FIELD_ROWS), :] = parts[s][
                k * FIELD_ROWS : (k + 1) * FIELD_ROWS, :
            ]
            for e in range(2):
                at = HELD * FIELD_ROWS + (e * HELD + k) * 8
                edge[pl.ds(member * EDGE_PITCH + 8 * e, 8), :] = parts[s][at : at + 8, :]

    def one(i, slot, obs, load):
        value = obs[i : i + 1]
        weight = obs[2 + i : 3 + i]
        index_f = obs[4 + i : 5 + i]
        index = jnp.broadcast_to(index_f.astype(jnp.int32), (MEMBERS, OBS))
        lane = index & 127
        chunk = index >> 7
        seen = jnp.zeros((MEMBERS, OBS), jnp.float32)
        for t in range(4):
            got = jnp.take_along_axis(load(t), lane, axis=1, mode="promise_in_bounds")
            seen = jnp.where(chunk == t, got, seen)
        mean = jnp.sum(seen, axis=0, keepdims=True) * (1.0 / MEMBERS)
        base = slot * SLAB
        slabs[i][pl.ds(base, MEMBERS), :] = weight * (seen - mean)
        slabs[i][pl.ds(base + MEMBERS, 1), :] = weight * (value - mean)
        slabs[i][pl.ds(base + MEMBERS + 1, 1), :] = index_f

    def body(c, carry):
        obs = obs_ref[c]
        for i in range(ROWS):
            one(i, c + 1, obs, lambda t: ens_ref[pl.ds(first_row(i, c) + 8 * t, MEMBERS, stride=PITCH), :])
        return carry

    lax.fori_loop(0, COLS, body, 0)
    for e, ref in enumerate((west_ref, east_ref)):
        obs = ref[...]
        for i in range(ROWS):
            one(
                i,
                e * (EXT_COLS - 1),
                obs,
                lambda t: edge[pl.ds(8 * e + 4 * i + t, MEMBERS, stride=EDGE_PITCH), :],
            )


def put_slab(slot, ref, base, source, pair, locs):
    t = lax.broadcasted_iota(jnp.int32, (8, OBS), 0)
    offset = (((t >> 1) - 1) * SIDE - (t & 1) * 8).astype(jnp.float32) - 3.5
    cell = ref[pl.ds(base + MEMBERS + 1, 1), :].astype(jnp.int32) & 255
    dy = (cell >> 4).astype(jnp.float32) + offset
    dx = (cell & 15).astype(jnp.float32) + offset
    locs[slot, 0:8, :] = jnp.exp(-(dy * dy) * INV_SCALE)
    locs[slot, 8:16, :] = jnp.exp(-(dx * dx) * INV_SCALE)
    scaled = ref[pl.ds(base, MEMBERS), :]
    source[slot] = scaled
    innovation = jnp.broadcast_to(ref[pl.ds(base + MEMBERS, 1), :], (8, OBS))
    high, low = split_bf16(jnp.concatenate([scaled, innovation], axis=0))
    pair[slot] = jnp.concatenate([high, low], axis=0)


def contribution(slot, di, dj, source, pair, locs):
    loc = locs[slot]
    base = source[slot]
    rows = []
    for a in range(2):
        for b in range(2):
            w = loc[2 * di + a : 2 * di + a + 1] * loc[8 + 2 * dj + b : 9 + 2 * dj + b]
            rows.append(w * base)
    high, low = split_bf16(jnp.concatenate(rows, axis=0))
    both = pair[slot]
    return lax.dot_general(
        jnp.concatenate([high, low], axis=1),
        jnp.concatenate([both, both], axis=1),
        (((1,), (1,)), ((), ())),
        preferred_element_type=jnp.float32,
    )


def own_gram_kernel(slab0_ref, slab1_ref, gram_ref, source, pair, locs):
    def put(c, carry):
        for i, ref in enumerate((slab0_ref, slab1_ref)):
            put_slab(i * EXT_COLS + c, ref, c * SLAB, source, pair, locs)
        return carry

    lax.fori_loop(0, EXT_COLS, put, 0)

    def one(c, carry):
        for i in range(ROWS):
            acc = jnp.zeros((POINTS * MEMBERS, 2 * WIDE), jnp.float32)
            for q in range(ROWS):
                for dj in range(3):
                    acc = acc + contribution(q * EXT_COLS + c + dj, q - i + 1, dj, source, pair, locs)
            for p in range(POINTS):
                gram_ref[pl.ds((i * COLS + c) * BLOCK_MAT + p * MAT, MEMBERS), 0 : 2 * WIDE] = acc[
                    p * MEMBERS : (p + 1) * MEMBERS
                ]
        return carry

    lax.fori_loop(0, COLS, one, 0)


def sym_product(left, right, out, finish):
    for tile in range(3):
        lo = 8 * tile
        for half in range(2):
            i0 = lo + 4 * half
            acc = [None] * 4
            for k in range(MEMBERS):
                row = right[k * MAT + lo : k * MAT + MEMBERS, :]
                for step in range(4):
                    at = (i0 + step) * MAT + k
                    term = left[at : at + 1, :] * row
                    acc[step] = term if acc[step] is None else acc[step] + term
            for step in range(4):
                i = i0 + step
                row = finish(acc[step], i, lo)
                out[i * MAT + lo : i * MAT + MEMBERS, :] = row
                for j in range(tile + 1, 3):
                    out[pl.ds(8 * j * MAT + i, 8, stride=MAT), :] = row[8 * (j - tile) : 8 * (j - tile) + 8]


def plain(row, i, lo):
    return row


def newton_step(row, i, lo):
    where = lax.broadcasted_iota(jnp.int32, row.shape, 0) + lo
    return jnp.where(where == i, 1.5, 0.0) - 0.5 * row


def analyze_kernel(m_ref, ens_ref, own_ref, above_ref, below_ref, *refs):
    outs = refs[:GROUPS]
    source, pair, locs, gram, ya, yb, za, zb, mm, drive, moved_ref = refs[GROUPS:]
    m = m_ref[0]

    def put(c, carry):
        put_slab(c, above_ref, c * SLAB, source, pair, locs)
        put_slab(EXT_COLS + c, below_ref, c * SLAB, source, pair, locs)
        return carry

    lax.fori_loop(0, EXT_COLS, put, 0)

    def one_gram(c, carry):
        for i in range(ROWS):
            acc = jnp.zeros((POINTS * MEMBERS, 2 * WIDE), jnp.float32)
            for dj in range(3):
                acc = acc + contribution(i * EXT_COLS + c + dj, 2 * i, dj, source, pair, locs)
            for p in range(POINTS):
                at = (i * COLS + c) * BLOCK_MAT + p * MAT
                gram[pl.ds(at, MEMBERS), 0 : 2 * WIDE] = (
                    own_ref[pl.ds(at, MEMBERS), 0 : 2 * WIDE] + acc[p * MEMBERS : (p + 1) * MEMBERS]
                )
        return carry

    lax.fori_loop(0, COLS, one_gram, 0)
    member = lax.broadcasted_iota(jnp.int32, (MEMBERS, 128), 0)
    squares = jnp.zeros((MEMBERS, 128), jnp.float32)
    for k in range(MEMBERS):
        turned = gram[pl.ds(k, 128, stride=MAT), :].T
        total = turned[0:WIDE] + turned[WIDE : 2 * WIDE]
        row = total[0:MEMBERS] + jnp.where(member == k, (MEMBERS - 1) / INFLATION_FACTOR, 0.0)
        drive[k : k + 1, :] = total[MEMBERS : MEMBERS + 1]
        ya[k * MAT : k * MAT + MEMBERS, :] = row
        squares = squares + row * row
    norm = jnp.sqrt(jnp.sum(squares, axis=0, keepdims=True))
    inverse = 1.0 / norm
    for k in range(MEMBERS):
        row = ya[k * MAT : k * MAT + MEMBERS, :] * inverse
        ya[k * MAT : k * MAT + MEMBERS, :] = row
        za[k * MAT : k * MAT + MEMBERS, :] = newton_step(row, k, 0)

    sym_product(ya, za, yb, plain)

    def two_steps(turn, carry):
        sym_product(za, yb, mm, newton_step)
        sym_product(yb, mm, ya, plain)
        sym_product(mm, za, zb, plain)
        sym_product(zb, ya, mm, newton_step)
        sym_product(ya, mm, yb, plain)
        sym_product(mm, zb, za, plain)
        return carry

    lax.fori_loop(0, (NS_ITERS - 2) // 2, two_steps, 0)
    sym_product(za, yb, mm, newton_step)
    sym_product(mm, za, zb, plain)

    scale = 1.0 / jnp.sqrt(norm)
    half_way = jnp.zeros((MEMBERS, 128), jnp.float32)
    for k in range(MEMBERS):
        half_way = half_way + zb[k * MAT : k * MAT + MEMBERS, :] * drive[k : k + 1, :]
    half_way = half_way * scale
    mean_w = jnp.zeros((MEMBERS, 128), jnp.float32)
    for k in range(MEMBERS):
        mean_w = mean_w + zb[k * MAT : k * MAT + MEMBERS, :] * half_way[k : k + 1]
    mean_w = mean_w * scale
    spread = scale * math.sqrt(MEMBERS - 1)
    blank = jnp.zeros((128 - 3 * MEMBERS, 128), jnp.float32)
    for k in range(MEMBERS):
        weight = mean_w + spread * zb[k * MAT : k * MAT + MEMBERS, :]
        high = weight.astype(jnp.bfloat16).astype(jnp.float32)
        gram[pl.ds(k, 128, stride=MAT), :] = jnp.concatenate(
            [high, high, weight - high, blank], axis=0
        ).T

    right_half = (lax.broadcasted_iota(jnp.int32, (MEMBERS, 128), 1) >> 3) & 1

    def one_update(c, carry):
        for i in range(ROWS):
            at = (i * COLS + c) * BLOCK_MAT
            first = first_row(i, c)
            ens = jnp.concatenate(
                [ens_ref[pl.ds(first + 8 * t, MEMBERS, stride=PITCH), :] for t in range(4)], axis=1
            )
            mean = jnp.sum(ens, axis=0, keepdims=True) * (1.0 / MEMBERS)
            anomaly = ens - mean
            high = anomaly.astype(jnp.bfloat16).astype(jnp.float32)
            low = anomaly - high
            stacked = jnp.concatenate(
                [high, low, high, jnp.zeros((128 - 3 * MEMBERS, VALS), jnp.float32)], axis=0
            ).astype(jnp.bfloat16)
            for a in range(2):
                values = jnp.concatenate(
                    [stacked[:, 128 * a : 128 * a + 128], stacked[:, 256 + 128 * a : 384 + 128 * a]], axis=1
                )
                weight = jnp.concatenate(
                    [gram[pl.ds(at + (2 * a + b) * MAT, MEMBERS), :] for b in range(2)], axis=0
                ).astype(jnp.bfloat16)
                moved = jnp.dot(weight, values, preferred_element_type=jnp.float32)
                for f in range(2):
                    part = moved[:, 128 * f : 128 * f + 128]
                    t = 2 * f + a
                    moved_tile = jnp.where(right_half == 1, part[MEMBERS:], part[:MEMBERS])
                    moved_ref[pl.ds(first + 8 * t, MEMBERS, stride=PITCH), :] = (
                        mean[:, 128 * t : 128 * t + 128] + moved_tile
                    )
        return carry

    lax.fori_loop(0, COLS, one_update, 0)
    for s in range(GROUPS):
        for k in range(HELD):
            start = ((m ^ s) * HELD + k) * PITCH
            outs[s][k * FIELD_ROWS : (k + 1) * FIELD_ROWS, :] = moved_ref[pl.ds(start, FIELD_ROWS), :]


def f32(*shape):
    return jax.ShapeDtypeStruct(shape, jnp.float32)


def tables(slots):
    return [
        pltpu.VMEM((slots, MEMBERS, OBS), jnp.float32),
        pltpu.VMEM((slots, 2 * WIDE, OBS), jnp.bfloat16),
        pltpu.VMEM((slots, 16, OBS), jnp.float32),
    ]


def vmem_call(kernel, out_shape, flops, args, scratch=()):
    places = [
        pl.BlockSpec(memory_space=pltpu.SMEM if x.dtype == jnp.int32 else pltpu.VMEM) for x in args
    ]
    return pl.pallas_call(
        kernel,
        out_shape=out_shape,
        in_specs=places,
        scratch_shapes=list(scratch),
        cost_estimate=pl.CostEstimate(flops=flops, bytes_accessed=0, transcendentals=0),
        compiler_params=pltpu.CompilerParams(vmem_limit_bytes=32 * 1024 * 1024),
    )(*args)


def swapped(x, s):
    return lax.ppermute(x, "member", [(a, a ^ s) for a in range(GROUPS)])


def shifted(x, axis, by):
    devices = lax.axis_size(axis)
    pairs = [(i, i + by) for i in range(devices) if 0 <= i + by < devices]
    return lax.ppermute(x, axis, pairs)


def local(ensemble, obs_value, obs_error, obs_index, obs_count):
    m = lax.axis_index("member").astype(jnp.int32)
    where = m.reshape(1)
    tiled = ensemble.reshape(HELD, ROWS, GROUPS, 2, 8, 4, 128).transpose(2, 0, 1, 3, 5, 4, 6)
    parts = []
    for s in range(GROUPS):
        to = m ^ s
        part = lax.dynamic_index_in_dim(tiled, to, 0, keepdims=False)
        edges = [
            lax.dynamic_slice_in_dim(ensemble, jnp.clip(at, 0, GROUPS * COLS - 1), 1, 2)
            for at in (to * COLS - 1, to * COLS + COLS)
        ]
        part = jnp.concatenate([x.reshape(-1, 128) for x in (part, *edges)], axis=0)
        parts.append(swapped(part, s) if s else part)

    slot = lax.broadcasted_iota(jnp.int32, (32, 1, OBS), 2)
    live = jnp.where(slot < obs_count[:, :, None], 1.0, 0.0).astype(jnp.float32)
    root_weight = jnp.sqrt(live / obs_error)
    pieces = [obs_value, root_weight, obs_index.astype(jnp.float32), jnp.zeros_like(obs_value)]
    packed = jnp.concatenate([x.reshape(COLS, ROWS, OBS) for x in pieces], axis=1)
    obs = lax.all_to_all(packed, "region", split_axis=0, concat_axis=0, tiled=True)

    west = shifted(obs[COLS - 1], "member", 1)
    east = shifted(obs[0], "member", -1)

    ens, slab0, slab1 = vmem_call(
        observe_kernel,
        (f32(MEMBERS * PITCH, 128), f32(SLAB_ROWS, OBS), f32(SLAB_ROWS, OBS)),
        10**9,
        [where, *parts, obs, west, east],
        [pltpu.VMEM((MEMBERS * EDGE_PITCH, 128), jnp.float32)],
    )

    below = shifted(slab0, "region", -1)
    above = shifted(slab1, "region", 1)

    own = vmem_call(
        own_gram_kernel,
        f32(BLOCKS * BLOCK_MAT, 128),
        4 * 10**9,
        [slab0, slab1],
        tables(ROWS * EXT_COLS),
    )

    square = pltpu.VMEM((MEMBERS * MAT, 128), jnp.float32)
    moved = vmem_call(
        analyze_kernel,
        [f32(HELD * FIELD_ROWS, 128)] * GROUPS,
        10**10,
        [where, ens, own, above, below],
        tables(ROWS * EXT_COLS)
        + [
            pltpu.VMEM((BLOCKS * BLOCK_MAT, 128), jnp.float32),
            square, square, square, square, square,
            pltpu.VMEM((MEMBERS, 128), jnp.float32),
            pltpu.VMEM((MEMBERS * PITCH, 128), jnp.float32),
        ],
    )

    result = jnp.zeros((HELD, ROWS, GROUPS, 2, 4, 8, 128), jnp.float32)
    for s in range(GROUPS):
        part = swapped(moved[s], s) if s else moved[s]
        part = part.reshape(HELD, ROWS, 1, 2, 4, 8, 128)
        result = lax.dynamic_update_slice_in_dim(result, part, m ^ s, 2)
    return result.transpose(0, 1, 2, 3, 5, 4, 6).reshape(HELD, ROWS, GROUPS * COLS, VALS)


def solution(mesh):
    return jax.shard_map(
        local,
        mesh=mesh,
        in_specs=(
            P("member", "region", None, None),
            P(None, ("member", "region"), None),
            P(None, ("member", "region"), None),
            P(None, ("member", "region"), None),
            P(None, ("member", "region")),
        ),
        out_specs=P("member", "region", None, None),
        check_vma=False,
    )
```

profile of v0, /device:TPU:33, one launch (start us, length us, event | category | flops | bytes accessed | tf_op | source)
XLA Modules:
  0.0 107.7 jit_solution(8895422002615457893)
XLA Ops:
  0.0 1.6 %constant_dynamic-slice_fusion.2 = (f32[3,2,1,2,8,4,128]{6,4,5,3,2,1,0:T(8,128)S(1)}, f32[3,2,1,2,8,4,128]{6,4,5,3,2,1,0:T(8,128)S(1)}, f32[3,2,1,2,8,4,128]{6,4...) fusion(f32[3,2,8,2,8,4,128]{6,4,5,3,2,1,0:T(8,128)} %bitcast.94, ...), kind=kLoop, calls=%fused_computation.22 | loop fusion | bytes 3145760 | tf_op jit(solution)/shard_map/dynamic-slice.7
  1.6 0.0 copy-start.2
  1.6 0.0 copy-start.3
  1.6 0.0 copy-start.4
  1.6 0.0 copy-start.1
  1.6 1.7 %constant_dynamic-slice_fusion.1 = (f32[3,2,1,512]{3,2,1,0:T(1,128)S(1)}, f32[3,2,1,512]{3,2,1,0:T(1,128)S(1)}, f32[3,2,1,512]{3,2,1,0:T(1,128)S(1)}, f32[3,2,1,...) fusion(f32[3,2,128,512]{3,2,1,0:T(8,128)} %param.5, ...), kind=kLoop, calls=%fused_computation.21 | loop fusion | bytes 393280 | tf_op jit(solution)/shard_map/dynamic_slice | solution.py:340
  3.4 0.8 collective-permute-start
  4.2 1.3 %collective-permute-start.1 = (f32[432,128]{1,0:T(8,128)S(1)}, f32[432,128]{1,0:T(8,128)S(1)}, u32[]{:S(2)}, u32[]{:S(2)}) collective-permute-start(f32[432,128]{1,0:T(8,128)S(1)} %pad_maximum_fusion.2), channel_id=1, source_target_pairs={{0,32},{16,48},{32,0},{48,16},{64,96},{80,112},{96,64},{112,80},{1... | collective-permute-start | bytes 663560 | tf_op jit(solution)/shard_map/ppermute | solution.py:322
  5.5 0.5 collective-permute-start.2
  6.0 0.1 fusion.1
  6.2 0.1 pad.3.clone
  6.2 0.7 maximum_maximum_fusion
  6.9 7.5 %all-to-all-start = ((f32[16,8,128]{2,1,0:T(8,128)}), f32[16,8,128]{2,1,0:T(8,128)S(1)}, u32[]{:S(2)}, u32[]{:S(2)}) async-start(f32[16,8,128]{2,1,0:T(8,128)} %maximum_maximum_fusion), calls=%async_computation | async-start | bytes 131072 | tf_op jit(solution)/shard_map/all_to_all | solution.py:351
  14.5 5.4 %all-to-all-done.refs_8_ = f32[16,8,128]{2,1,0:T(8,128)S(1)} async-done(((f32[16,8,128]{2,1,0:T(8,128)}), f32[16,8,128]{2,1,0:T(8,128)S(1)}, u32[]{:S(2)}, u32[]{:S(2)}) %all-to-all-start) | async-done | bytes 65568 | tf_op jit(solution)/shard_map/all_to_all | solution.py:351
  19.9 4.6 %collective-permute-start.7 = (f32[8,128]{1,0:T(8,128)S(1)}, f32[8,128]{1,0:T(8,128)S(1)}, u32[]{:S(2)}, u32[]{:S(2)}) collective-permute-start(f32[8,128]{1,0:T(8,128)S(1)} %get-tuple-element.52), channel_id=1, source_target_pairs={{0,16},{16,32},{32,48},{48,64},{64,80},{80,96},{96,112},{1,17},{17... | collective-permute-start | bytes 12296 | tf_op jit(solution)/shard_map/ppermute | solution.py:328
  24.5 1.9 %collective-permute-start.8 = (f32[8,128]{1,0:T(8,128)S(1)}, f32[8,128]{1,0:T(8,128)S(1)}, u32[]{:S(2)}, u32[]{:S(2)}) collective-permute-start(f32[8,128]{1,0:T(8,128)S(1)} %get-tuple-element.51), channel_id=1, source_target_pairs={{16,0},{32,16},{48,32},{64,48},{80,64},{96,80},{112,96},{17,1},{33... | collective-permute-start | bytes 12296 | tf_op jit(solution)/shard_map/ppermute | solution.py:328
  26.4 0.0 collective-permute-done.7.refs_9_
  26.5 2.5 %collective-permute-start.3 = (f32[432,128]{1,0:T(8,128)S(1)}, f32[432,128]{1,0:T(8,128)S(1)}, u32[]{:S(2)}, u32[]{:S(2)}) collective-permute-start(f32[432,128]{1,0:T(8,128)S(1)} %pad_maximum_fusion.4), channel_id=1, source_target_pairs={{0,64},{16,80},{32,96},{48,112},{64,0},{80,16},{96,32},{112,48},{1... | collective-permute-start | bytes 663560 | tf_op jit(solution)/shard_map/ppermute | solution.py:322
  29.0 0.4 collective-permute-done.8.refs_10_
  29.4 1.6 %collective-permute-start.4 = (f32[432,128]{1,0:T(8,128)S(1)}, f32[432,128]{1,0:T(8,128)S(1)}, u32[]{:S(2)}, u32[]{:S(2)}) collective-permute-start(f32[432,128]{1,0:T(8,128)S(1)} %pad_maximum_fusion.5), channel_id=1, source_target_pairs={{0,80},{16,64},{32,112},{48,96},{64,16},{80,0},{96,48},{112,32},{1... | collective-permute-start | bytes 663560 | tf_op jit(solution)/shard_map/ppermute | solution.py:322
  31.0 1.8 %collective-permute-start.5 = (f32[432,128]{1,0:T(8,128)S(1)}, f32[432,128]{1,0:T(8,128)S(1)}, u32[]{:S(2)}, u32[]{:S(2)}) collective-permute-start(f32[432,128]{1,0:T(8,128)S(1)} %pad_maximum_fusion.6), channel_id=1, source_target_pairs={{0,96},{16,112},{32,64},{48,80},{64,32},{80,48},{96,0},{112,16},{1... | collective-permute-start | bytes 663560 | tf_op jit(solution)/shard_map/ppermute | solution.py:322
  32.8 0.0 collective-permute-done.1.refs_2_
  32.8 2.3 %collective-permute-start.6 = (f32[432,128]{1,0:T(8,128)S(1)}, f32[432,128]{1,0:T(8,128)S(1)}, u32[]{:S(2)}, u32[]{:S(2)}) collective-permute-start(f32[432,128]{1,0:T(8,128)S(1)} %pad_maximum_fusion.7), channel_id=1, source_target_pairs={{0,112},{16,96},{32,80},{48,64},{64,48},{80,32},{96,16},{112,0},{1... | collective-permute-start | bytes 663560 | tf_op jit(solution)/shard_map/ppermute | solution.py:322
  35.1 0.0 collective-permute-done.3.refs_4_
  35.2 4.9 %collective-permute-done.4.refs_5_ = f32[432,128]{1,0:T(8,128)S(1)} collective-permute-done((f32[432,128]{1,0:T(8,128)S(1)}, f32[432,128]{1,0:T(8,128)S(1)}, u32[]{:S(2)}, u32[]{:S(2)}) %collective-permute-start.4) | collective-permute-done | bytes 221216 | tf_op jit(solution)/shard_map/ppermute | solution.py:322
  40.0 4.8 %collective-permute-done.5.refs_6_ = f32[432,128]{1,0:T(8,128)S(1)} collective-permute-done((f32[432,128]{1,0:T(8,128)S(1)}, f32[432,128]{1,0:T(8,128)S(1)}, u32[]{:S(2)}, u32[]{:S(2)}) %collective-permute-start.5) | collective-permute-done | bytes 221216 | tf_op jit(solution)/shard_map/ppermute | solution.py:322
  44.9 4.7 %collective-permute-done.6.refs_7_ = f32[432,128]{1,0:T(8,128)S(1)} collective-permute-done((f32[432,128]{1,0:T(8,128)S(1)}, f32[432,128]{1,0:T(8,128)S(1)}, u32[]{:S(2)}, u32[]{:S(2)}) %collective-permute-start.6) | collective-permute-done | bytes 221216 | tf_op jit(solution)/shard_map/ppermute | solution.py:322
  49.6 2.4 %shard_map.58 = (f32[3168,128]{1,0:T(8,128)S(1)}, f32[472,128]{1,0:T(8,128)S(1)}, f32[472,128]{1,0:T(8,128)S(1)}) custom-call(s32[1]{0:T(128)} %bitcast.m_ref, f32[432,128]{1,0:T(8,128)S(1)} %pad_maximum_fusion.refs_0_, f32[432,128]{1,0:T(8,128)S(1)} %collective-permute-done.refs_1_, f32[432,128]{1,0:T(8,128)S(1)} %collective-permute-done.1.refs_2_, ...), custom_call_target="tpu_custom_call" | custom-call | flops 1000000000 | tf_op jit(solution)/shard_map/pallas_call | solution.py:311
  52.0 3.7 %collective-permute-start.10 = (f32[472,128]{1,0:T(8,128)S(1)}, f32[472,128]{1,0:T(8,128)S(1)}, u32[]{:S(2)}, u32[]{:S(2)}) collective-permute-start(f32[472,128]{1,0:T(8,128)S(1)} %get-tuple-element.17.slab0_ref), channel_id=1, source_target_pairs={{1,0},{2,1},{3,2},{4,3},{5,4},{6,5},{7,6},{8,7},{9,8},{10,9},{11,1... | collective-permute-start | bytes 725000 | tf_op jit(solution)/shard_map/ppermute | solution.py:328
  55.7 1.9 %collective-permute-start.9 = (f32[472,128]{1,0:T(8,128)S(1)}, f32[472,128]{1,0:T(8,128)S(1)}, u32[]{:S(2)}, u32[]{:S(2)}) collective-permute-start(f32[472,128]{1,0:T(8,128)S(1)} %get-tuple-element.18.slab1_ref), channel_id=1, source_target_pairs={{0,1},{1,2},{2,3},{3,4},{4,5},{5,6},{6,7},{7,8},{8,9},{9,10},{10,1... | collective-permute-start | bytes 725000 | tf_op jit(solution)/shard_map/ppermute | solution.py:328
  57.7 5.5 %shard_map.59.own_ref = f32[3584,128]{1,0:T(8,128)S(1)} custom-call(f32[472,128]{1,0:T(8,128)S(1)} %get-tuple-element.17.slab0_ref, f32[472,128]{1,0:T(8,128)S(1)} %get-tuple-element.18.slab1_ref), custom_call_target="tpu_custom_call" | custom-call | flops 4000000000 | tf_op jit(solution)/shard_map/pallas_call | solution.py:311
  63.2 3.3 %collective-permute-done.9.above_ref = f32[472,128]{1,0:T(8,128)S(1)} collective-permute-done((f32[472,128]{1,0:T(8,128)S(1)}, f32[472,128]{1,0:T(8,128)S(1)}, u32[]{:S(2)}, u32[]{:S(2)}) %collective-permute-start.9) | collective-permute-done | bytes 241696 | tf_op jit(solution)/shard_map/ppermute | solution.py:328
  66.5 12.7 %shard_map.60 = (f32[384,128]{1,0:T(8,128)S(1)}, f32[384,128]{1,0:T(8,128)S(1)}, f32[384,128]{1,0:T(8,128)S(1)}, f32[384,128]{1,0:T(8,128)S(1)}, f32[384,128]{1,...) custom-call(s32[1]{0:T(128)} %bitcast.m_ref, ...), custom_call_target="tpu_custom_call" | custom-call | flops 10000000000 | tf_op jit(solution)/shard_map/pallas_call | solution.py:311
  79.2 1.6 %collective-permute-start.11 = (f32[384,128]{1,0:T(8,128)S(1)}, f32[384,128]{1,0:T(8,128)S(1)}, u32[]{:S(2)}, u32[]{:S(2)}) collective-permute-start(f32[384,128]{1,0:T(8,128)S(1)} %get-tuple-element.20), channel_id=1, source_target_pairs={{0,16},{16,0},{32,48},{48,32},{64,80},{80,64},{96,112},{112,96},{1... | collective-permute-start | bytes 589832 | tf_op jit(solution)/shard_map/ppermute | solution.py:322
  80.8 1.3 %collective-permute-start.12 = (f32[384,128]{1,0:T(8,128)S(1)}, f32[384,128]{1,0:T(8,128)S(1)}, u32[]{:S(2)}, u32[]{:S(2)}) collective-permute-start(f32[384,128]{1,0:T(8,128)S(1)} %get-tuple-element.21), channel_id=1, source_target_pairs={{0,32},{16,48},{32,0},{48,16},{64,96},{80,112},{96,64},{112,80},{1... | collective-permute-start | bytes 589832 | tf_op jit(solution)/shard_map/ppermute | solution.py:322
  82.1 0.4 collective-permute-start.13
  82.5 2.5 %collective-permute-start.14 = (f32[384,128]{1,0:T(8,128)S(1)}, f32[384,128]{1,0:T(8,128)S(1)}, u32[]{:S(2)}, u32[]{:S(2)}) collective-permute-start(f32[384,128]{1,0:T(8,128)S(1)} %get-tuple-element.23), channel_id=1, source_target_pairs={{0,64},{16,80},{32,96},{48,112},{64,0},{80,16},{96,32},{112,48},{1... | collective-permute-start | bytes 589832 | tf_op jit(solution)/shard_map/ppermute | solution.py:322
  85.0 0.7 collective-permute-start.15
  85.8 0.2 broadcast_in_dim.12
  86.0 1.5 %collective-permute-start.16 = (f32[384,128]{1,0:T(8,128)S(1)}, f32[384,128]{1,0:T(8,128)S(1)}, u32[]{:S(2)}, u32[]{:S(2)}) collective-permute-start(f32[384,128]{1,0:T(8,128)S(1)} %get-tuple-element.25), channel_id=1, source_target_pairs={{0,96},{16,112},{32,64},{48,80},{64,32},{80,48},{96,0},{112,16},{1... | collective-permute-start | bytes 589832 | tf_op jit(solution)/shard_map/ppermute | solution.py:322
  87.5 2.4 %collective-permute-start.17 = (f32[384,128]{1,0:T(8,128)S(1)}, f32[384,128]{1,0:T(8,128)S(1)}, u32[]{:S(2)}, u32[]{:S(2)}) collective-permute-start(f32[384,128]{1,0:T(8,128)S(1)} %get-tuple-element.26), channel_id=1, source_target_pairs={{0,112},{16,96},{32,80},{48,64},{64,48},{80,32},{96,16},{112,0},{1... | collective-permute-start | bytes 589832 | tf_op jit(solution)/shard_map/ppermute | solution.py:322
  89.9 2.5 %collective-permute-done.13 = f32[384,128]{1,0:T(8,128)S(1)} collective-permute-done((f32[384,128]{1,0:T(8,128)S(1)}, f32[384,128]{1,0:T(8,128)S(1)}, u32[]{:S(2)}, u32[]{:S(2)}) %collective-permute-start.13) | collective-permute-done | bytes 196640 | tf_op jit(solution)/shard_map/ppermute | solution.py:322
  92.5 4.2 %collective-permute-done.14 = f32[384,128]{1,0:T(8,128)S(1)} collective-permute-done((f32[384,128]{1,0:T(8,128)S(1)}, f32[384,128]{1,0:T(8,128)S(1)}, u32[]{:S(2)}, u32[]{:S(2)}) %collective-permute-start.14) | collective-permute-done | bytes 196640 | tf_op jit(solution)/shard_map/ppermute | solution.py:322
  96.7 4.5 %collective-permute-done.15 = f32[384,128]{1,0:T(8,128)S(1)} collective-permute-done((f32[384,128]{1,0:T(8,128)S(1)}, f32[384,128]{1,0:T(8,128)S(1)}, u32[]{:S(2)}, u32[]{:S(2)}) %collective-permute-start.15) | collective-permute-done | bytes 196640 | tf_op jit(solution)/shard_map/ppermute | solution.py:322
  101.3 0.8 collective-permute-done.16
  102.1 4.5 %collective-permute-done.17 = f32[384,128]{1,0:T(8,128)S(1)} collective-permute-done((f32[384,128]{1,0:T(8,128)S(1)}, f32[384,128]{1,0:T(8,128)S(1)}, u32[]{:S(2)}, u32[]{:S(2)}) %collective-permute-start.17) | collective-permute-done | bytes 196640 | tf_op jit(solution)/shard_map/ppermute | solution.py:322
  106.6 0.0 copy-start
  106.6 1.1 %copy-done = f32[3,2,8,2,4,8,128]{6,5,4,3,2,1,0:T(8,128)} copy-done((f32[3,2,8,2,4,8,128]{6,5,4,3,2,1,0:T(8,128)}, f32[3,2,8,2,4,8,128]{6,5,4,3,2,1,0:T(8,128)S(1)}, u32[]{:S(2)}) %copy-start) | copy-done | bytes 1572888
  (28 shorter events, 0.3 us)
Async XLA Ops:
  1.6 4.4 %copy-start.2 = (s32[32,1,128]{2,1,0:T(1,128)S(1)}, s32[32,1,128]{2,1,0:T(1,128)}, u32[]{:S(2)}) copy-start(s32[32,1,128]{2,1,0:T(1,128)} %param.8) | copy-start | bytes 49156
  1.6 4.4 %copy-start.3 = (f32[32,1,128]{2,1,0:T(1,128)S(1)}, f32[32,1,128]{2,1,0:T(1,128)}, u32[]{:S(2)}) copy-start(f32[32,1,128]{2,1,0:T(1,128)} %param.7) | copy-start | bytes 49156
  1.6 4.4 %copy-start.4 = (s32[32,1]{0,1:T(1,128)S(1)}, s32[32,1]{0,1:T(1,128)}, u32[]{:S(2)}) copy-start(s32[32,1]{0,1:T(1,128)} %param.9) | copy-start | bytes 388
  1.6 4.6 %copy-start.1 = (f32[32,1,128]{2,1,0:T(1,128)S(1)}, f32[32,1,128]{2,1,0:T(1,128)}, u32[]{:S(2)}) copy-start(f32[32,1,128]{2,1,0:T(1,128)} %param.6) | copy-start | bytes 49156
  3.4 27.6 %collective-permute-start = (f32[432,128]{1,0:T(8,128)S(1)}, f32[432,128]{1,0:T(8,128)S(1)}, u32[]{:S(2)}, u32[]{:S(2)}) collective-permute-start(f32[432,128]{1,0:T(8,128)S(1)} %pad_maximum_fusion.1), channel_id=1, source_target_pairs={{0,16},{16,0},{32,48},{48,32},{64,80},{80,64},{96,112},{112,96},{1... | collective-permute-start | bytes 663560 | tf_op jit(solution)/shard_map/ppermute | solution.py:322
  4.2 28.6 %collective-permute-start.1 = (f32[432,128]{1,0:T(8,128)S(1)}, f32[432,128]{1,0:T(8,128)S(1)}, u32[]{:S(2)}, u32[]{:S(2)}) collective-permute-start(f32[432,128]{1,0:T(8,128)S(1)} %pad_maximum_fusion.2), channel_id=1, source_target_pairs={{0,32},{16,48},{32,0},{48,16},{64,96},{80,112},{96,64},{112,80},{1... | collective-permute-start | bytes 663560 | tf_op jit(solution)/shard_map/ppermute | solution.py:322
  5.5 29.7 %collective-permute-start.2 = (f32[432,128]{1,0:T(8,128)S(1)}, f32[432,128]{1,0:T(8,128)S(1)}, u32[]{:S(2)}, u32[]{:S(2)}) collective-permute-start(f32[432,128]{1,0:T(8,128)S(1)} %pad_maximum_fusion.3), channel_id=1, source_target_pairs={{0,48},{16,32},{32,16},{48,0},{64,112},{80,96},{96,80},{112,64},{1... | collective-permute-start | bytes 663560 | tf_op jit(solution)/shard_map/ppermute | solution.py:322
  6.9 12.9 %all-to-all-start = ((f32[16,8,128]{2,1,0:T(8,128)}), f32[16,8,128]{2,1,0:T(8,128)S(1)}, u32[]{:S(2)}, u32[]{:S(2)}) async-start(f32[16,8,128]{2,1,0:T(8,128)} %maximum_maximum_fusion), calls=%async_computation | async-start | bytes 131072 | tf_op jit(solution)/shard_map/all_to_all | solution.py:351
  19.9 6.6 %collective-permute-start.7 = (f32[8,128]{1,0:T(8,128)S(1)}, f32[8,128]{1,0:T(8,128)S(1)}, u32[]{:S(2)}, u32[]{:S(2)}) collective-permute-start(f32[8,128]{1,0:T(8,128)S(1)} %get-tuple-element.52), channel_id=1, source_target_pairs={{0,16},{16,32},{32,48},{48,64},{64,80},{80,96},{96,112},{1,17},{17... | collective-permute-start | bytes 12296 | tf_op jit(solution)/shard_map/ppermute | solution.py:328
  24.5 4.9 %collective-permute-start.8 = (f32[8,128]{1,0:T(8,128)S(1)}, f32[8,128]{1,0:T(8,128)S(1)}, u32[]{:S(2)}, u32[]{:S(2)}) collective-permute-start(f32[8,128]{1,0:T(8,128)S(1)} %get-tuple-element.51), channel_id=1, source_target_pairs={{16,0},{32,16},{48,32},{64,48},{80,64},{96,80},{112,96},{17,1},{33... | collective-permute-start | bytes 12296 | tf_op jit(solution)/shard_map/ppermute | solution.py:328
  26.5 8.7 %collective-permute-start.3 = (f32[432,128]{1,0:T(8,128)S(1)}, f32[432,128]{1,0:T(8,128)S(1)}, u32[]{:S(2)}, u32[]{:S(2)}) collective-permute-start(f32[432,128]{1,0:T(8,128)S(1)} %pad_maximum_fusion.4), channel_id=1, source_target_pairs={{0,64},{16,80},{32,96},{48,112},{64,0},{80,16},{96,32},{112,48},{1... | collective-permute-start | bytes 663560 | tf_op jit(solution)/shard_map/ppermute | solution.py:322
  29.4 10.6 %collective-permute-start.4 = (f32[432,128]{1,0:T(8,128)S(1)}, f32[432,128]{1,0:T(8,128)S(1)}, u32[]{:S(2)}, u32[]{:S(2)}) collective-permute-start(f32[432,128]{1,0:T(8,128)S(1)} %pad_maximum_fusion.5), channel_id=1, source_target_pairs={{0,80},{16,64},{32,112},{48,96},{64,16},{80,0},{96,48},{112,32},{1... | collective-permute-start | bytes 663560 | tf_op jit(solution)/shard_map/ppermute | solution.py:322
  31.0 13.9 %collective-permute-start.5 = (f32[432,128]{1,0:T(8,128)S(1)}, f32[432,128]{1,0:T(8,128)S(1)}, u32[]{:S(2)}, u32[]{:S(2)}) collective-permute-start(f32[432,128]{1,0:T(8,128)S(1)} %pad_maximum_fusion.6), channel_id=1, source_target_pairs={{0,96},{16,112},{32,64},{48,80},{64,32},{80,48},{96,0},{112,16},{1... | collective-permute-start | bytes 663560 | tf_op jit(solution)/shard_map/ppermute | solution.py:322
  32.8 16.8 %collective-permute-start.6 = (f32[432,128]{1,0:T(8,128)S(1)}, f32[432,128]{1,0:T(8,128)S(1)}, u32[]{:S(2)}, u32[]{:S(2)}) collective-permute-start(f32[432,128]{1,0:T(8,128)S(1)} %pad_maximum_fusion.7), channel_id=1, source_target_pairs={{0,112},{16,96},{32,80},{48,64},{64,48},{80,32},{96,16},{112,0},{1... | collective-permute-start | bytes 663560 | tf_op jit(solution)/shard_map/ppermute | solution.py:322
  52.0 11.2 %collective-permute-start.10 = (f32[472,128]{1,0:T(8,128)S(1)}, f32[472,128]{1,0:T(8,128)S(1)}, u32[]{:S(2)}, u32[]{:S(2)}) collective-permute-start(f32[472,128]{1,0:T(8,128)S(1)} %get-tuple-element.17.slab0_ref), channel_id=1, source_target_pairs={{1,0},{2,1},{3,2},{4,3},{5,4},{6,5},{7,6},{8,7},{9,8},{10,9},{11,1... | collective-permute-start | bytes 725000 | tf_op jit(solution)/shard_map/ppermute | solution.py:328
  55.7 10.8 %collective-permute-start.9 = (f32[472,128]{1,0:T(8,128)S(1)}, f32[472,128]{1,0:T(8,128)S(1)}, u32[]{:S(2)}, u32[]{:S(2)}) collective-permute-start(f32[472,128]{1,0:T(8,128)S(1)} %get-tuple-element.18.slab1_ref), channel_id=1, source_target_pairs={{0,1},{1,2},{2,3},{3,4},{4,5},{5,6},{6,7},{7,8},{8,9},{9,10},{10,1... | collective-permute-start | bytes 725000 | tf_op jit(solution)/shard_map/ppermute | solution.py:328
  79.2 6.8 %collective-permute-start.11 = (f32[384,128]{1,0:T(8,128)S(1)}, f32[384,128]{1,0:T(8,128)S(1)}, u32[]{:S(2)}, u32[]{:S(2)}) collective-permute-start(f32[384,128]{1,0:T(8,128)S(1)} %get-tuple-element.20), channel_id=1, source_target_pairs={{0,16},{16,0},{32,48},{48,32},{64,80},{80,64},{96,112},{112,96},{1... | collective-permute-start | bytes 589832 | tf_op jit(solution)/shard_map/ppermute | solution.py:322
  80.8 6.7 %collective-permute-start.12 = (f32[384,128]{1,0:T(8,128)S(1)}, f32[384,128]{1,0:T(8,128)S(1)}, u32[]{:S(2)}, u32[]{:S(2)}) collective-permute-start(f32[384,128]{1,0:T(8,128)S(1)} %get-tuple-element.21), channel_id=1, source_target_pairs={{0,32},{16,48},{32,0},{48,16},{64,96},{80,112},{96,64},{112,80},{1... | collective-permute-start | bytes 589832 | tf_op jit(solution)/shard_map/ppermute | solution.py:322
  82.1 10.4 %collective-permute-start.13 = (f32[384,128]{1,0:T(8,128)S(1)}, f32[384,128]{1,0:T(8,128)S(1)}, u32[]{:S(2)}, u32[]{:S(2)}) collective-permute-start(f32[384,128]{1,0:T(8,128)S(1)} %get-tuple-element.22), channel_id=1, source_target_pairs={{0,48},{16,32},{32,16},{48,0},{64,112},{80,96},{96,80},{112,64},{1... | collective-permute-start | bytes 589832 | tf_op jit(solution)/shard_map/ppermute | solution.py:322
  82.5 14.2 %collective-permute-start.14 = (f32[384,128]{1,0:T(8,128)S(1)}, f32[384,128]{1,0:T(8,128)S(1)}, u32[]{:S(2)}, u32[]{:S(2)}) collective-permute-start(f32[384,128]{1,0:T(8,128)S(1)} %get-tuple-element.23), channel_id=1, source_target_pairs={{0,64},{16,80},{32,96},{48,112},{64,0},{80,16},{96,32},{112,48},{1... | collective-permute-start | bytes 589832 | tf_op jit(solution)/shard_map/ppermute | solution.py:322
  85.0 16.2 %collective-permute-start.15 = (f32[384,128]{1,0:T(8,128)S(1)}, f32[384,128]{1,0:T(8,128)S(1)}, u32[]{:S(2)}, u32[]{:S(2)}) collective-permute-start(f32[384,128]{1,0:T(8,128)S(1)} %get-tuple-element.24), channel_id=1, source_target_pairs={{0,80},{16,64},{32,112},{48,96},{64,16},{80,0},{96,48},{112,32},{1... | collective-permute-start | bytes 589832 | tf_op jit(solution)/shard_map/ppermute | solution.py:322
  86.0 16.1 %collective-permute-start.16 = (f32[384,128]{1,0:T(8,128)S(1)}, f32[384,128]{1,0:T(8,128)S(1)}, u32[]{:S(2)}, u32[]{:S(2)}) collective-permute-start(f32[384,128]{1,0:T(8,128)S(1)} %get-tuple-element.25), channel_id=1, source_target_pairs={{0,96},{16,112},{32,64},{48,80},{64,32},{80,48},{96,0},{112,16},{1... | collective-permute-start | bytes 589832 | tf_op jit(solution)/shard_map/ppermute | solution.py:322
  87.5 19.1 %collective-permute-start.17 = (f32[384,128]{1,0:T(8,128)S(1)}, f32[384,128]{1,0:T(8,128)S(1)}, u32[]{:S(2)}, u32[]{:S(2)}) collective-permute-start(f32[384,128]{1,0:T(8,128)S(1)} %get-tuple-element.26), channel_id=1, source_target_pairs={{0,112},{16,96},{32,80},{48,64},{64,48},{80,32},{96,16},{112,0},{1... | collective-permute-start | bytes 589832 | tf_op jit(solution)/shard_map/ppermute | solution.py:322
  106.6 1.1 %copy-start = (f32[3,2,8,2,4,8,128]{6,5,4,3,2,1,0:T(8,128)}, f32[3,2,8,2,4,8,128]{6,5,4,3,2,1,0:T(8,128)S(1)}, u32[]{:S(2)}) copy-start(f32[3,2,8,2,4,8,128]{6,5,4,3,2,1,0:T(8,128)S(1)} %constant_dynamic-update-slice_fusion) | copy-start | bytes 4718596
where the time goes:
time: 108 us
  starting transfers between devices  40.9 us (38%)
  waiting for transfers between devices  40.1 us (37%)
  Pallas kernels  20.5 us (19%)
  local copies, waits for them, and re-layouts  4.86 us (5%)
    ppermute x14, waiting for transfers between devices, swapped(): return lax.ppermute(x, 'member', [(a, a ^ s) for a in range(GROUPS)])  31 us
    ppermute x14, starting transfers between devices, swapped(): return lax.ppermute(x, 'member', [(a, a ^ s) for a in range(GROUPS)])  21.3 us
    pallas_call x3, Pallas kernels, vmem_call(): pl.pallas_call(kernel, out_shape=out_shape, in_specs=places, scratch_shap...  20.5 us
    ppermute x4, starting transfers between devices, shifted(): return lax.ppermute(x, axis, pairs)  12.2 us
    all_to_all x1, starting transfers between devices, local(): lax.all_to_all(packed, 'region', split_axis=0, concat_axis=0, tiled=True)  7.51 us
    all_to_all x1, waiting for transfers between devices, local(): lax.all_to_all(packed, 'region', split_axis=0, concat_axis=0, tiled=True)  5.37 us
    ppermute x4, waiting for transfers between devices, shifted(): return lax.ppermute(x, axis, pairs)  3.75 us
  transfers between devices with their start and end apart: 19, of which 11 were waited for; matrix products, arithmetic and copies ran while one was open for 1% of the time, Pallas kernels for 5%

commit v1 on v0

--- a/solution.py
+++ b/solution.py
@@ -27,6 +27,7 @@
 PITCH = FIELD_ROWS + 4
 SLAB = 26
 WIDE = 32
+STACK = 80
 SLAB_ROWS = 472
 EDGE_PITCH = 20
 MAT = MEMBERS + 4
@@ -81,7 +82,7 @@
             one(i, c + 1, obs, lambda t: ens_ref[pl.ds(first_row(i, c) + 8 * t, MEMBERS, stride=PITCH), :])
         return carry
 
-    lax.fori_loop(0, COLS, body, 0)
+    lax.fori_loop(0, COLS, body, 0, unroll=2)
     for e, ref in enumerate((west_ref, east_ref)):
         obs = ref[...]
         for i in range(ROWS):
@@ -126,7 +127,7 @@
     )
 
 
-def own_gram_kernel(slab0_ref, slab1_ref, gram_ref, source, pair, locs):
+def own_gram_kernel(slab0_ref, slab1_ref, ens_ref, gram_ref, stack_ref, mean_ref, source, pair, locs):
     def put(c, carry):
         for i, ref in enumerate((slab0_ref, slab1_ref)):
             put_slab(i * EXT_COLS + c, ref, c * SLAB, source, pair, locs)
@@ -146,7 +147,25 @@
                 ]
         return carry
 
-    lax.fori_loop(0, COLS, one, 0)
+    lax.fori_loop(0, COLS, one, 0, unroll=4)
+
+    def stack(c, carry):
+        for i in range(ROWS):
+            block = i * COLS + c
+            for t in range(4):
+                ens = ens_ref[pl.ds(first_row(i, c) + 8 * t, MEMBERS, stride=PITCH), :]
+                mean = jnp.sum(ens, axis=0, keepdims=True) * (1.0 / MEMBERS)
+                mean_ref[pl.ds(block * 4 + t, 1), :] = mean
+                anomaly = ens - mean
+                high = anomaly.astype(jnp.bfloat16).astype(jnp.float32)
+                rows = jnp.concatenate(
+                    [high, anomaly - high, high, jnp.zeros((STACK - 3 * MEMBERS, 128), jnp.float32)], axis=0
+                )
+                f, a = t // 2, t % 2
+                stack_ref[2 * block + a, :, 128 * f : 128 * f + 128] = rows.astype(jnp.bfloat16)
+        return carry
+
+    lax.fori_loop(0, COLS, stack, 0, unroll=2)
 
 
 def sym_product(left, right, out, finish):
@@ -178,7 +197,7 @@
     return jnp.where(where == i, 1.5, 0.0) - 0.5 * row
 
 
-def analyze_kernel(m_ref, ens_ref, own_ref, above_ref, below_ref, *refs):
+def analyze_kernel(m_ref, stack_ref, mean_ref, own_ref, above_ref, below_ref, *refs):
     outs = refs[:GROUPS]
     source, pair, locs, gram, ya, yb, za, zb, mm, drive, moved_ref = refs[GROUPS:]
     m = m_ref[0]
@@ -202,7 +221,7 @@
                 )
         return carry
 
-    lax.fori_loop(0, COLS, one_gram, 0)
+    lax.fori_loop(0, COLS, one_gram, 0, unroll=8)
     member = lax.broadcasted_iota(jnp.int32, (MEMBERS, 128), 0)
     squares = jnp.zeros((MEMBERS, 128), jnp.float32)
     for k in range(MEMBERS):
@@ -258,19 +277,9 @@
         for i in range(ROWS):
             at = (i * COLS + c) * BLOCK_MAT
             first = first_row(i, c)
-            ens = jnp.concatenate(
-                [ens_ref[pl.ds(first + 8 * t, MEMBERS, stride=PITCH), :] for t in range(4)], axis=1
-            )
-            mean = jnp.sum(ens, axis=0, keepdims=True) * (1.0 / MEMBERS)
-            anomaly = ens - mean
-            high = anomaly.astype(jnp.bfloat16).astype(jnp.float32)
-            low = anomaly - high
-            stacked = jnp.concatenate(
-                [high, low, high, jnp.zeros((128 - 3 * MEMBERS, VALS), jnp.float32)], axis=0
-            ).astype(jnp.bfloat16)
             for a in range(2):
                 values = jnp.concatenate(
-                    [stacked[:, 128 * a : 128 * a + 128], stacked[:, 256 + 128 * a : 384 + 128 * a]], axis=1
+                    [stack_ref[2 * (i * COLS + c) + a], jnp.zeros((128 - STACK, 256), jnp.bfloat16)], axis=0
                 )
                 weight = jnp.concatenate(
                     [gram[pl.ds(at + (2 * a + b) * MAT, MEMBERS), :] for b in range(2)], axis=0
@@ -281,11 +290,11 @@
                     t = 2 * f + a
                     moved_tile = jnp.where(right_half == 1, part[MEMBERS:], part[:MEMBERS])
                     moved_ref[pl.ds(first + 8 * t, MEMBERS, stride=PITCH), :] = (
-                        mean[:, 128 * t : 128 * t + 128] + moved_tile
+                        mean_ref[pl.ds((i * COLS + c) * 4 + t, 1), :] + moved_tile
                     )
         return carry
 
-    lax.fori_loop(0, COLS, one_update, 0)
+    lax.fori_loop(0, COLS, one_update, 0, unroll=8)
     for s in range(GROUPS):
         for k in range(HELD):
             start = ((m ^ s) * HELD + k) * PITCH
@@ -364,11 +373,15 @@
     below = shifted(slab0, "region", -1)
     above = shifted(slab1, "region", 1)
 
-    own = vmem_call(
+    own, stack, mean = vmem_call(
         own_gram_kernel,
-        f32(BLOCKS * BLOCK_MAT, 128),
+        (
+            f32(BLOCKS * BLOCK_MAT, 128),
+            jax.ShapeDtypeStruct((2 * BLOCKS, STACK, 256), jnp.bfloat16),
+            f32(BLOCKS * 4, 128),
+        ),
         4 * 10**9,
-        [slab0, slab1],
+        [slab0, slab1, ens],
         tables(ROWS * EXT_COLS),
     )
 
@@ -377,7 +390,7 @@
         analyze_kernel,
         [f32(HELD * FIELD_ROWS, 128)] * GROUPS,
         10**10,
-        [where, ens, own, above, below],
+        [where, stack, mean, own, above, below],
         tables(ROWS * EXT_COLS)
         + [
             pltpu.VMEM((BLOCKS * BLOCK_MAT, 128), jnp.float32),

time: 108 us -> 103 us (0.954)
  Pallas kernels: 20.5 us -> 14.1 us
  waiting for transfers between devices: 40.1 us -> 41.6 us
    pallas_call x3, Pallas kernels: 20.5 us -> 14.1 us  [vmem_call(): pl.pallas_call(kernel, out_shape=out_shape, in_specs=places, scratch_shap...]
    ppermute x4, waiting for transfers between devices: 3.75 us -> 5.2 us  [shifted(): return lax.ppermute(x, axis, pairs)]
  transfers between devices with their start and end apart: 19 -> 19, of which waited for: 11 -> 11; matrix products, arithmetic and copies ran while one was open for 1% -> 1% of each run, Pallas kernels for 5% -> 4%
where the time goes in v1:
time: 103 us
  waiting for transfers between devices  41.6 us (40%)
  starting transfers between devices  40.9 us (40%)
  Pallas kernels  14.1 us (14%)
  local copies, waits for them, and re-layouts  4.86 us (5%)
    ppermute x14, waiting for transfers between devices, swapped(): return lax.ppermute(x, 'member', [(a, a ^ s) for a in range(GROUPS)])  31 us
    ppermute x14, starting transfers between devices, swapped(): return lax.ppermute(x, 'member', [(a, a ^ s) for a in range(GROUPS)])  21.3 us
    pallas_call x3, Pallas kernels, vmem_call(): pl.pallas_call(kernel, out_shape=out_shape, in_specs=places, scratch_shap...  14.1 us
    ppermute x4, starting transfers between devices, shifted(): return lax.ppermute(x, axis, pairs)  12.2 us
    all_to_all x1, starting transfers between devices, local(): lax.all_to_all(packed, 'region', split_axis=0, concat_axis=0, tiled=True)  7.51 us
    all_to_all x1, waiting for transfers between devices, local(): lax.all_to_all(packed, 'region', split_axis=0, concat_axis=0, tiled=True)  5.37 us
    ppermute x4, waiting for transfers between devices, shifted(): return lax.ppermute(x, axis, pairs)  5.2 us
  transfers between devices with their start and end apart: 19, of which 11 were waited for; matrix products, arithmetic and copies ran while one was open for 1% of the time, Pallas kernels for 4%

profile of v1, /device:TPU:33, one launch (start us, length us, event | category | flops | bytes accessed | tf_op | source)
XLA Modules:
  0.0 102.8 jit_solution(10011958446726419976)
XLA Ops:
  0.0 1.6 %constant_dynamic-slice_fusion.2 = (f32[3,2,1,2,8,4,128]{6,4,5,3,2,1,0:T(8,128)S(1)}, f32[3,2,1,2,8,4,128]{6,4,5,3,2,1,0:T(8,128)S(1)}, f32[3,2,1,2,8,4,128]{6,4...) fusion(f32[3,2,8,2,8,4,128]{6,4,5,3,2,1,0:T(8,128)} %bitcast.94, ...), kind=kLoop, calls=%fused_computation.22 | loop fusion | bytes 3145760 | tf_op jit(solution)/shard_map/dynamic-slice.7
  1.6 0.0 copy-start.2
  1.6 0.0 copy-start.3
  1.6 0.0 copy-start.4
  1.6 0.0 copy-start.1
  1.6 1.7 %constant_dynamic-slice_fusion.1 = (f32[3,2,1,512]{3,2,1,0:T(1,128)S(1)}, f32[3,2,1,512]{3,2,1,0:T(1,128)S(1)}, f32[3,2,1,512]{3,2,1,0:T(1,128)S(1)}, f32[3,2,1,...) fusion(f32[3,2,128,512]{3,2,1,0:T(8,128)} %param.5, ...), kind=kLoop, calls=%fused_computation.21 | loop fusion | bytes 393280 | tf_op jit(solution)/shard_map/dynamic_slice | solution.py:349
  3.4 0.8 collective-permute-start
  4.2 1.3 %collective-permute-start.1 = (f32[432,128]{1,0:T(8,128)S(1)}, f32[432,128]{1,0:T(8,128)S(1)}, u32[]{:S(2)}, u32[]{:S(2)}) collective-permute-start(f32[432,128]{1,0:T(8,128)S(1)} %pad_maximum_fusion.2), channel_id=1, source_target_pairs={{0,32},{16,48},{32,0},{48,16},{64,96},{80,112},{96,64},{112,80},{1... | collective-permute-start | bytes 663560 | tf_op jit(solution)/shard_map/ppermute | solution.py:331
  5.5 0.5 collective-permute-start.2
  6.0 0.1 fusion.1
  6.2 0.1 pad.3.clone
  6.2 0.7 maximum_maximum_fusion
  6.9 7.5 %all-to-all-start = ((f32[16,8,128]{2,1,0:T(8,128)}), f32[16,8,128]{2,1,0:T(8,128)S(1)}, u32[]{:S(2)}, u32[]{:S(2)}) async-start(f32[16,8,128]{2,1,0:T(8,128)} %maximum_maximum_fusion), calls=%async_computation | async-start | bytes 131072 | tf_op jit(solution)/shard_map/all_to_all | solution.py:360
  14.5 5.4 %all-to-all-done.refs_8_ = f32[16,8,128]{2,1,0:T(8,128)S(1)} async-done(((f32[16,8,128]{2,1,0:T(8,128)}), f32[16,8,128]{2,1,0:T(8,128)S(1)}, u32[]{:S(2)}, u32[]{:S(2)}) %all-to-all-start) | async-done | bytes 65568 | tf_op jit(solution)/shard_map/all_to_all | solution.py:360
  19.9 4.6 %collective-permute-start.7 = (f32[8,128]{1,0:T(8,128)S(1)}, f32[8,128]{1,0:T(8,128)S(1)}, u32[]{:S(2)}, u32[]{:S(2)}) collective-permute-start(f32[8,128]{1,0:T(8,128)S(1)} %get-tuple-element.58), channel_id=1, source_target_pairs={{0,16},{16,32},{32,48},{48,64},{64,80},{80,96},{96,112},{1,17},{17... | collective-permute-start | bytes 12296 | tf_op jit(solution)/shard_map/ppermute | solution.py:337
  24.5 1.9 %collective-permute-start.8 = (f32[8,128]{1,0:T(8,128)S(1)}, f32[8,128]{1,0:T(8,128)S(1)}, u32[]{:S(2)}, u32[]{:S(2)}) collective-permute-start(f32[8,128]{1,0:T(8,128)S(1)} %get-tuple-element.57), channel_id=1, source_target_pairs={{16,0},{32,16},{48,32},{64,48},{80,64},{96,80},{112,96},{17,1},{33... | collective-permute-start | bytes 12296 | tf_op jit(solution)/shard_map/ppermute | solution.py:337
  26.4 0.0 collective-permute-done.7.refs_9_
  26.5 2.5 %collective-permute-start.3 = (f32[432,128]{1,0:T(8,128)S(1)}, f32[432,128]{1,0:T(8,128)S(1)}, u32[]{:S(2)}, u32[]{:S(2)}) collective-permute-start(f32[432,128]{1,0:T(8,128)S(1)} %pad_maximum_fusion.4), channel_id=1, source_target_pairs={{0,64},{16,80},{32,96},{48,112},{64,0},{80,16},{96,32},{112,48},{1... | collective-permute-start | bytes 663560 | tf_op jit(solution)/shard_map/ppermute | solution.py:331
  29.0 0.4 collective-permute-done.8.refs_10_
  29.4 1.6 %collective-permute-start.4 = (f32[432,128]{1,0:T(8,128)S(1)}, f32[432,128]{1,0:T(8,128)S(1)}, u32[]{:S(2)}, u32[]{:S(2)}) collective-permute-start(f32[432,128]{1,0:T(8,128)S(1)} %pad_maximum_fusion.5), channel_id=1, source_target_pairs={{0,80},{16,64},{32,112},{48,96},{64,16},{80,0},{96,48},{112,32},{1... | collective-permute-start | bytes 663560 | tf_op jit(solution)/shard_map/ppermute | solution.py:331
  31.0 1.8 %collective-permute-start.5 = (f32[432,128]{1,0:T(8,128)S(1)}, f32[432,128]{1,0:T(8,128)S(1)}, u32[]{:S(2)}, u32[]{:S(2)}) collective-permute-start(f32[432,128]{1,0:T(8,128)S(1)} %pad_maximum_fusion.6), channel_id=1, source_target_pairs={{0,96},{16,112},{32,64},{48,80},{64,32},{80,48},{96,0},{112,16},{1... | collective-permute-start | bytes 663560 | tf_op jit(solution)/shard_map/ppermute | solution.py:331
  32.8 0.0 collective-permute-done.1.refs_2_
  32.8 2.3 %collective-permute-start.6 = (f32[432,128]{1,0:T(8,128)S(1)}, f32[432,128]{1,0:T(8,128)S(1)}, u32[]{:S(2)}, u32[]{:S(2)}) collective-permute-start(f32[432,128]{1,0:T(8,128)S(1)} %pad_maximum_fusion.7), channel_id=1, source_target_pairs={{0,112},{16,96},{32,80},{48,64},{64,48},{80,32},{96,16},{112,0},{1... | collective-permute-start | bytes 663560 | tf_op jit(solution)/shard_map/ppermute | solution.py:331
  35.1 0.0 collective-permute-done.3.refs_4_
  35.2 4.9 %collective-permute-done.4.refs_5_ = f32[432,128]{1,0:T(8,128)S(1)} collective-permute-done((f32[432,128]{1,0:T(8,128)S(1)}, f32[432,128]{1,0:T(8,128)S(1)}, u32[]{:S(2)}, u32[]{:S(2)}) %collective-permute-start.4) | collective-permute-done | bytes 221216 | tf_op jit(solution)/shard_map/ppermute | solution.py:331
  40.0 4.8 %collective-permute-done.5.refs_6_ = f32[432,128]{1,0:T(8,128)S(1)} collective-permute-done((f32[432,128]{1,0:T(8,128)S(1)}, f32[432,128]{1,0:T(8,128)S(1)}, u32[]{:S(2)}, u32[]{:S(2)}) %collective-permute-start.5) | collective-permute-done | bytes 221216 | tf_op jit(solution)/shard_map/ppermute | solution.py:331
  44.9 4.7 %collective-permute-done.6.refs_7_ = f32[432,128]{1,0:T(8,128)S(1)} collective-permute-done((f32[432,128]{1,0:T(8,128)S(1)}, f32[432,128]{1,0:T(8,128)S(1)}, u32[]{:S(2)}, u32[]{:S(2)}) %collective-permute-start.6) | collective-permute-done | bytes 221216 | tf_op jit(solution)/shard_map/ppermute | solution.py:331
  49.6 1.6 %shard_map.58 = (f32[3168,128]{1,0:T(8,128)S(1)}, f32[472,128]{1,0:T(8,128)S(1)}, f32[472,128]{1,0:T(8,128)S(1)}) custom-call(s32[1]{0:T(128)} %bitcast.m_ref, f32[432,128]{1,0:T(8,128)S(1)} %pad_maximum_fusion.refs_0_, f32[432,128]{1,0:T(8,128)S(1)} %collective-permute-done.refs_1_, f32[432,128]{1,0:T(8,128)S(1)} %collective-permute-done.1.refs_2_, ...), custom_call_target="tpu_custom_call" | custom-call | flops 1000000000 | tf_op jit(solution)/shard_map/pallas_call | solution.py:320
  51.2 3.7 %collective-permute-start.10 = (f32[472,128]{1,0:T(8,128)S(1)}, f32[472,128]{1,0:T(8,128)S(1)}, u32[]{:S(2)}, u32[]{:S(2)}) collective-permute-start(f32[472,128]{1,0:T(8,128)S(1)} %get-tuple-element.19.slab0_ref), channel_id=1, source_target_pairs={{1,0},{2,1},{3,2},{4,3},{5,4},{6,5},{7,6},{8,7},{9,8},{10,9},{11,1... | collective-permute-start | bytes 725000 | tf_op jit(solution)/shard_map/ppermute | solution.py:337
  54.9 1.9 %collective-permute-start.9 = (f32[472,128]{1,0:T(8,128)S(1)}, f32[472,128]{1,0:T(8,128)S(1)}, u32[]{:S(2)}, u32[]{:S(2)}) collective-permute-start(f32[472,128]{1,0:T(8,128)S(1)} %get-tuple-element.20.slab1_ref), channel_id=1, source_target_pairs={{0,1},{1,2},{2,3},{3,4},{4,5},{5,6},{6,7},{7,8},{8,9},{9,10},{10,1... | collective-permute-start | bytes 725000 | tf_op jit(solution)/shard_map/ppermute | solution.py:337
  56.9 4.0 %shard_map.59 = (f32[3584,128]{1,0:T(8,128)S(1)}, bf16[64,80,256]{2,1,0:T(8,128)(2,1)S(1)}, f32[128,128]{1,0:T(8,128)S(1)}) custom-call(f32[472,128]{1,0:T(8,128)S(1)} %get-tuple-element.19.slab0_ref, f32[472,128]{1,0:T(8,128)S(1)} %get-tuple-element.20.slab1_ref, f32[3168,128]{1,0:T(8,128)S(1)} %get-tuple-element.21.ens_ref), custom_call_target="tpu_custom_call" | custom-call | flops 4000000000 | tf_op jit(solution)/shard_map/pallas_call | solution.py:320
  60.9 4.8 %collective-permute-done.9.above_ref = f32[472,128]{1,0:T(8,128)S(1)} collective-permute-done((f32[472,128]{1,0:T(8,128)S(1)}, f32[472,128]{1,0:T(8,128)S(1)}, u32[]{:S(2)}, u32[]{:S(2)}) %collective-permute-start.9) | collective-permute-done | bytes 241696 | tf_op jit(solution)/shard_map/ppermute | solution.py:337
  65.7 8.5 %shard_map.60 = (f32[384,128]{1,0:T(8,128)S(1)}, f32[384,128]{1,0:T(8,128)S(1)}, f32[384,128]{1,0:T(8,128)S(1)}, f32[384,128]{1,0:T(8,128)S(1)}, f32[384,128]{1,...) custom-call(s32[1]{0:T(128)} %bitcast.m_ref, ...), custom_call_target="tpu_custom_call" | custom-call | flops 10000000000 | tf_op jit(solution)/shard_map/pallas_call | solution.py:320
  74.2 1.6 %collective-permute-start.11 = (f32[384,128]{1,0:T(8,128)S(1)}, f32[384,128]{1,0:T(8,128)S(1)}, u32[]{:S(2)}, u32[]{:S(2)}) collective-permute-start(f32[384,128]{1,0:T(8,128)S(1)} %get-tuple-element.26), channel_id=1, source_target_pairs={{0,16},{16,0},{32,48},{48,32},{64,80},{80,64},{96,112},{112,96},{1... | collective-permute-start | bytes 589832 | tf_op jit(solution)/shard_map/ppermute | solution.py:331
  75.8 1.3 %collective-permute-start.12 = (f32[384,128]{1,0:T(8,128)S(1)}, f32[384,128]{1,0:T(8,128)S(1)}, u32[]{:S(2)}, u32[]{:S(2)}) collective-permute-start(f32[384,128]{1,0:T(8,128)S(1)} %get-tuple-element.27), channel_id=1, source_target_pairs={{0,32},{16,48},{32,0},{48,16},{64,96},{80,112},{96,64},{112,80},{1... | collective-permute-start | bytes 589832 | tf_op jit(solution)/shard_map/ppermute | solution.py:331
  77.1 0.4 collective-permute-start.13
  77.6 2.5 %collective-permute-start.14 = (f32[384,128]{1,0:T(8,128)S(1)}, f32[384,128]{1,0:T(8,128)S(1)}, u32[]{:S(2)}, u32[]{:S(2)}) collective-permute-start(f32[384,128]{1,0:T(8,128)S(1)} %get-tuple-element.29), channel_id=1, source_target_pairs={{0,64},{16,80},{32,96},{48,112},{64,0},{80,16},{96,32},{112,48},{1... | collective-permute-start | bytes 589832 | tf_op jit(solution)/shard_map/ppermute | solution.py:331
  80.1 0.8 collective-permute-start.15
  80.8 0.2 broadcast_in_dim.12
  81.1 1.4 %collective-permute-start.16 = (f32[384,128]{1,0:T(8,128)S(1)}, f32[384,128]{1,0:T(8,128)S(1)}, u32[]{:S(2)}, u32[]{:S(2)}) collective-permute-start(f32[384,128]{1,0:T(8,128)S(1)} %get-tuple-element.31), channel_id=1, source_target_pairs={{0,96},{16,112},{32,64},{48,80},{64,32},{80,48},{96,0},{112,16},{1... | collective-permute-start | bytes 589832 | tf_op jit(solution)/shard_map/ppermute | solution.py:331
  82.5 2.4 %collective-permute-start.17 = (f32[384,128]{1,0:T(8,128)S(1)}, f32[384,128]{1,0:T(8,128)S(1)}, u32[]{:S(2)}, u32[]{:S(2)}) collective-permute-start(f32[384,128]{1,0:T(8,128)S(1)} %get-tuple-element.32), channel_id=1, source_target_pairs={{0,112},{16,96},{32,80},{48,64},{64,48},{80,32},{96,16},{112,0},{1... | collective-permute-start | bytes 589832 | tf_op jit(solution)/shard_map/ppermute | solution.py:331
  85.0 2.5 %collective-permute-done.13 = f32[384,128]{1,0:T(8,128)S(1)} collective-permute-done((f32[384,128]{1,0:T(8,128)S(1)}, f32[384,128]{1,0:T(8,128)S(1)}, u32[]{:S(2)}, u32[]{:S(2)}) %collective-permute-start.13) | collective-permute-done | bytes 196640 | tf_op jit(solution)/shard_map/ppermute | solution.py:331
  87.5 4.2 %collective-permute-done.14 = f32[384,128]{1,0:T(8,128)S(1)} collective-permute-done((f32[384,128]{1,0:T(8,128)S(1)}, f32[384,128]{1,0:T(8,128)S(1)}, u32[]{:S(2)}, u32[]{:S(2)}) %collective-permute-start.14) | collective-permute-done | bytes 196640 | tf_op jit(solution)/shard_map/ppermute | solution.py:331
  91.8 4.5 %collective-permute-done.15 = f32[384,128]{1,0:T(8,128)S(1)} collective-permute-done((f32[384,128]{1,0:T(8,128)S(1)}, f32[384,128]{1,0:T(8,128)S(1)}, u32[]{:S(2)}, u32[]{:S(2)}) %collective-permute-start.15) | collective-permute-done | bytes 196640 | tf_op jit(solution)/shard_map/ppermute | solution.py:331
  96.3 0.8 collective-permute-done.16
  97.2 4.5 %collective-permute-done.17 = f32[384,128]{1,0:T(8,128)S(1)} collective-permute-done((f32[384,128]{1,0:T(8,128)S(1)}, f32[384,128]{1,0:T(8,128)S(1)}, u32[]{:S(2)}, u32[]{:S(2)}) %collective-permute-start.17) | collective-permute-done | bytes 196640 | tf_op jit(solution)/shard_map/ppermute | solution.py:331
  101.6 0.0 copy-start
  101.6 1.1 %copy-done = f32[3,2,8,2,4,8,128]{6,5,4,3,2,1,0:T(8,128)} copy-done((f32[3,2,8,2,4,8,128]{6,5,4,3,2,1,0:T(8,128)}, f32[3,2,8,2,4,8,128]{6,5,4,3,2,1,0:T(8,128)S(1)}, u32[]{:S(2)}) %copy-start) | copy-done | bytes 1572888
  (28 shorter events, 0.3 us)
Async XLA Ops:
  1.6 4.4 %copy-start.2 = (s32[32,1,128]{2,1,0:T(1,128)S(1)}, s32[32,1,128]{2,1,0:T(1,128)}, u32[]{:S(2)}) copy-start(s32[32,1,128]{2,1,0:T(1,128)} %param.8) | copy-start | bytes 49156
  1.6 4.4 %copy-start.3 = (f32[32,1,128]{2,1,0:T(1,128)S(1)}, f32[32,1,128]{2,1,0:T(1,128)}, u32[]{:S(2)}) copy-start(f32[32,1,128]{2,1,0:T(1,128)} %param.7) | copy-start | bytes 49156
  1.6 4.4 %copy-start.4 = (s32[32,1]{0,1:T(1,128)S(1)}, s32[32,1]{0,1:T(1,128)}, u32[]{:S(2)}) copy-start(s32[32,1]{0,1:T(1,128)} %param.9) | copy-start | bytes 388
  1.6 4.6 %copy-start.1 = (f32[32,1,128]{2,1,0:T(1,128)S(1)}, f32[32,1,128]{2,1,0:T(1,128)}, u32[]{:S(2)}) copy-start(f32[32,1,128]{2,1,0:T(1,128)} %param.6) | copy-start | bytes 49156
  3.4 27.6 %collective-permute-start = (f32[432,128]{1,0:T(8,128)S(1)}, f32[432,128]{1,0:T(8,128)S(1)}, u32[]{:S(2)}, u32[]{:S(2)}) collective-permute-start(f32[432,128]{1,0:T(8,128)S(1)} %pad_maximum_fusion.1), channel_id=1, source_target_pairs={{0,16},{16,0},{32,48},{48,32},{64,80},{80,64},{96,112},{112,96},{1... | collective-permute-start | bytes 663560 | tf_op jit(solution)/shard_map/ppermute | solution.py:331
  4.2 28.6 %collective-permute-start.1 = (f32[432,128]{1,0:T(8,128)S(1)}, f32[432,128]{1,0:T(8,128)S(1)}, u32[]{:S(2)}, u32[]{:S(2)}) collective-permute-start(f32[432,128]{1,0:T(8,128)S(1)} %pad_maximum_fusion.2), channel_id=1, source_target_pairs={{0,32},{16,48},{32,0},{48,16},{64,96},{80,112},{96,64},{112,80},{1... | collective-permute-start | bytes 663560 | tf_op jit(solution)/shard_map/ppermute | solution.py:331
  5.5 29.7 %collective-permute-start.2 = (f32[432,128]{1,0:T(8,128)S(1)}, f32[432,128]{1,0:T(8,128)S(1)}, u32[]{:S(2)}, u32[]{:S(2)}) collective-permute-start(f32[432,128]{1,0:T(8,128)S(1)} %pad_maximum_fusion.3), channel_id=1, source_target_pairs={{0,48},{16,32},{32,16},{48,0},{64,112},{80,96},{96,80},{112,64},{1... | collective-permute-start | bytes 663560 | tf_op jit(solution)/shard_map/ppermute | solution.py:331
  6.9 12.9 %all-to-all-start = ((f32[16,8,128]{2,1,0:T(8,128)}), f32[16,8,128]{2,1,0:T(8,128)S(1)}, u32[]{:S(2)}, u32[]{:S(2)}) async-start(f32[16,8,128]{2,1,0:T(8,128)} %maximum_maximum_fusion), calls=%async_computation | async-start | bytes 131072 | tf_op jit(solution)/shard_map/all_to_all | solution.py:360
  19.9 6.6 %collective-permute-start.7 = (f32[8,128]{1,0:T(8,128)S(1)}, f32[8,128]{1,0:T(8,128)S(1)}, u32[]{:S(2)}, u32[]{:S(2)}) collective-permute-start(f32[8,128]{1,0:T(8,128)S(1)} %get-tuple-element.58), channel_id=1, source_target_pairs={{0,16},{16,32},{32,48},{48,64},{64,80},{80,96},{96,112},{1,17},{17... | collective-permute-start | bytes 12296 | tf_op jit(solution)/shard_map/ppermute | solution.py:337
  24.5 4.9 %collective-permute-start.8 = (f32[8,128]{1,0:T(8,128)S(1)}, f32[8,128]{1,0:T(8,128)S(1)}, u32[]{:S(2)}, u32[]{:S(2)}) collective-permute-start(f32[8,128]{1,0:T(8,128)S(1)} %get-tuple-element.57), channel_id=1, source_target_pairs={{16,0},{32,16},{48,32},{64,48},{80,64},{96,80},{112,96},{17,1},{33... | collective-permute-start | bytes 12296 | tf_op jit(solution)/shard_map/ppermute | solution.py:337
  26.5 8.7 %collective-permute-start.3 = (f32[432,128]{1,0:T(8,128)S(1)}, f32[432,128]{1,0:T(8,128)S(1)}, u32[]{:S(2)}, u32[]{:S(2)}) collective-permute-start(f32[432,128]{1,0:T(8,128)S(1)} %pad_maximum_fusion.4), channel_id=1, source_target_pairs={{0,64},{16,80},{32,96},{48,112},{64,0},{80,16},{96,32},{112,48},{1... | collective-permute-start | bytes 663560 | tf_op jit(solution)/shard_map/ppermute | solution.py:331
  29.4 10.6 %collective-permute-start.4 = (f32[432,128]{1,0:T(8,128)S(1)}, f32[432,128]{1,0:T(8,128)S(1)}, u32[]{:S(2)}, u32[]{:S(2)}) collective-permute-start(f32[432,128]{1,0:T(8,128)S(1)} %pad_maximum_fusion.5), channel_id=1, source_target_pairs={{0,80},{16,64},{32,112},{48,96},{64,16},{80,0},{96,48},{112,32},{1... | collective-permute-start | bytes 663560 | tf_op jit(solution)/shard_map/ppermute | solution.py:331
  31.0 13.9 %collective-permute-start.5 = (f32[432,128]{1,0:T(8,128)S(1)}, f32[432,128]{1,0:T(8,128)S(1)}, u32[]{:S(2)}, u32[]{:S(2)}) collective-permute-start(f32[432,128]{1,0:T(8,128)S(1)} %pad_maximum_fusion.6), channel_id=1, source_target_pairs={{0,96},{16,112},{32,64},{48,80},{64,32},{80,48},{96,0},{112,16},{1... | collective-permute-start | bytes 663560 | tf_op jit(solution)/shard_map/ppermute | solution.py:331
  32.8 16.8 %collective-permute-start.6 = (f32[432,128]{1,0:T(8,128)S(1)}, f32[432,128]{1,0:T(8,128)S(1)}, u32[]{:S(2)}, u32[]{:S(2)}) collective-permute-start(f32[432,128]{1,0:T(8,128)S(1)} %pad_maximum_fusion.7), channel_id=1, source_target_pairs={{0,112},{16,96},{32,80},{48,64},{64,48},{80,32},{96,16},{112,0},{1... | collective-permute-start | bytes 663560 | tf_op jit(solution)/shard_map/ppermute | solution.py:331
  51.2 9.7 %collective-permute-start.10 = (f32[472,128]{1,0:T(8,128)S(1)}, f32[472,128]{1,0:T(8,128)S(1)}, u32[]{:S(2)}, u32[]{:S(2)}) collective-permute-start(f32[472,128]{1,0:T(8,128)S(1)} %get-tuple-element.19.slab0_ref), channel_id=1, source_target_pairs={{1,0},{2,1},{3,2},{4,3},{5,4},{6,5},{7,6},{8,7},{9,8},{10,9},{11,1... | collective-permute-start | bytes 725000 | tf_op jit(solution)/shard_map/ppermute | solution.py:337
  54.9 10.8 %collective-permute-start.9 = (f32[472,128]{1,0:T(8,128)S(1)}, f32[472,128]{1,0:T(8,128)S(1)}, u32[]{:S(2)}, u32[]{:S(2)}) collective-permute-start(f32[472,128]{1,0:T(8,128)S(1)} %get-tuple-element.20.slab1_ref), channel_id=1, source_target_pairs={{0,1},{1,2},{2,3},{3,4},{4,5},{5,6},{6,7},{7,8},{8,9},{9,10},{10,1... | collective-permute-start | bytes 725000 | tf_op jit(solution)/shard_map/ppermute | solution.py:337
  74.2 6.8 %collective-permute-start.11 = (f32[384,128]{1,0:T(8,128)S(1)}, f32[384,128]{1,0:T(8,128)S(1)}, u32[]{:S(2)}, u32[]{:S(2)}) collective-permute-start(f32[384,128]{1,0:T(8,128)S(1)} %get-tuple-element.26), channel_id=1, source_target_pairs={{0,16},{16,0},{32,48},{48,32},{64,80},{80,64},{96,112},{112,96},{1... | collective-permute-start | bytes 589832 | tf_op jit(solution)/shard_map/ppermute | solution.py:331
  75.8 6.7 %collective-permute-start.12 = (f32[384,128]{1,0:T(8,128)S(1)}, f32[384,128]{1,0:T(8,128)S(1)}, u32[]{:S(2)}, u32[]{:S(2)}) collective-permute-start(f32[384,128]{1,0:T(8,128)S(1)} %get-tuple-element.27), channel_id=1, source_target_pairs={{0,32},{16,48},{32,0},{48,16},{64,96},{80,112},{96,64},{112,80},{1... | collective-permute-start | bytes 589832 | tf_op jit(solution)/shard_map/ppermute | solution.py:331
  77.1 10.4 %collective-permute-start.13 = (f32[384,128]{1,0:T(8,128)S(1)}, f32[384,128]{1,0:T(8,128)S(1)}, u32[]{:S(2)}, u32[]{:S(2)}) collective-permute-start(f32[384,128]{1,0:T(8,128)S(1)} %get-tuple-element.28), channel_id=1, source_target_pairs={{0,48},{16,32},{32,16},{48,0},{64,112},{80,96},{96,80},{112,64},{1... | collective-permute-start | bytes 589832 | tf_op jit(solution)/shard_map/ppermute | solution.py:331
  77.6 14.2 %collective-permute-start.14 = (f32[384,128]{1,0:T(8,128)S(1)}, f32[384,128]{1,0:T(8,128)S(1)}, u32[]{:S(2)}, u32[]{:S(2)}) collective-permute-start(f32[384,128]{1,0:T(8,128)S(1)} %get-tuple-element.29), channel_id=1, source_target_pairs={{0,64},{16,80},{32,96},{48,112},{64,0},{80,16},{96,32},{112,48},{1... | collective-permute-start | bytes 589832 | tf_op jit(solution)/shard_map/ppermute | solution.py:331
  80.1 16.2 %collective-permute-start.15 = (f32[384,128]{1,0:T(8,128)S(1)}, f32[384,128]{1,0:T(8,128)S(1)}, u32[]{:S(2)}, u32[]{:S(2)}) collective-permute-start(f32[384,128]{1,0:T(8,128)S(1)} %get-tuple-element.30), channel_id=1, source_target_pairs={{0,80},{16,64},{32,112},{48,96},{64,16},{80,0},{96,48},{112,32},{1... | collective-permute-start | bytes 589832 | tf_op jit(solution)/shard_map/ppermute | solution.py:331
  81.1 16.1 %collective-permute-start.16 = (f32[384,128]{1,0:T(8,128)S(1)}, f32[384,128]{1,0:T(8,128)S(1)}, u32[]{:S(2)}, u32[]{:S(2)}) collective-permute-start(f32[384,128]{1,0:T(8,128)S(1)} %get-tuple-element.31), channel_id=1, source_target_pairs={{0,96},{16,112},{32,64},{48,80},{64,32},{80,48},{96,0},{112,16},{1... | collective-permute-start | bytes 589832 | tf_op jit(solution)/shard_map/ppermute | solution.py:331
  82.5 19.1 %collective-permute-start.17 = (f32[384,128]{1,0:T(8,128)S(1)}, f32[384,128]{1,0:T(8,128)S(1)}, u32[]{:S(2)}, u32[]{:S(2)}) collective-permute-start(f32[384,128]{1,0:T(8,128)S(1)} %get-tuple-element.32), channel_id=1, source_target_pairs={{0,112},{16,96},{32,80},{48,64},{64,48},{80,32},{96,16},{112,0},{1... | collective-permute-start | bytes 589832 | tf_op jit(solution)/shard_map/ppermute | solution.py:331
  101.6 1.1 %copy-start = (f32[3,2,8,2,4,8,128]{6,5,4,3,2,1,0:T(8,128)}, f32[3,2,8,2,4,8,128]{6,5,4,3,2,1,0:T(8,128)S(1)}, u32[]{:S(2)}) copy-start(f32[3,2,8,2,4,8,128]{6,5,4,3,2,1,0:T(8,128)S(1)} %constant_dynamic-update-slice_fusion) | copy-start | bytes 4718596

commit v2 on v1

--- a/solution.py
+++ b/solution.py
@@ -30,6 +30,7 @@
 STACK = 80
 SLAB_ROWS = 472
 EDGE_PITCH = 20
+PART_ROWS = HELD * (FIELD_ROWS + 16)
 MAT = MEMBERS + 4
 BLOCK_MAT = POINTS * MAT
 
@@ -44,9 +45,39 @@
     return high, low
 
 
+def pack_kernel(m_ref, ens_ref, *refs):
+    outs = refs[:GROUPS]
+    stage, sems = refs[GROUPS:]
+    m = m_ref[0]
+    tiles = GROUPS * 8
+    chunk_rows = tiles * 8
+    copies = []
+    for n in range(HELD * ROWS):
+        copy = pltpu.make_async_copy(
+            ens_ref.at[pl.ds(n * chunk_rows, chunk_rows), :],
+            stage.at[pl.ds(n * chunk_rows, chunk_rows), :],
+            sems.at[n],
+        )
+        copy.start()
+        copies.append(copy)
+
+    for n in range(HELD * ROWS):
+        k, i = n // ROWS, n % ROWS
+        copies[n].wait()
+        for s in range(GROUPS):
+            to = m ^ s
+            start = pl.multiple_of(n * chunk_rows + to * 64, 64)
+            outs[s][n * 64 : n * 64 + 64, :] = stage[pl.ds(start, 64), :]
+            before = jnp.maximum(2 * to - 1, 0) * 32 + 7
+            after = jnp.minimum(2 * to + 2, 2 * GROUPS - 1) * 32
+            for e, at in enumerate((before, after)):
+                row = HELD * FIELD_ROWS + (e * HELD + k) * 8 + 4 * i
+                outs[s][row : row + 4, :] = stage[pl.ds(n * chunk_rows + at, 4, stride=8), :]
+
+
 def observe_kernel(m_ref, *refs):
     parts = refs[:GROUPS]
-    obs_ref, west_ref, east_ref, ens_ref, slab0_ref, slab1_ref, edge = refs[GROUPS:]
+    obs_ref, ens_ref, slab0_ref, slab1_ref, edge = refs[GROUPS:]
     slabs = (slab0_ref, slab1_ref)
     m = m_ref[0]
     for s in range(GROUPS):
@@ -83,8 +114,8 @@
         return carry
 
     lax.fori_loop(0, COLS, body, 0, unroll=2)
-    for e, ref in enumerate((west_ref, east_ref)):
-        obs = ref[...]
+    for e, source in enumerate((COLS - 1, 0)):
+        obs = obs_ref[source, 8:16, :]
         for i in range(ROWS):
             one(
                 i,
@@ -337,36 +368,45 @@
     return lax.ppermute(x, axis, pairs)
 
 
+def edge_columns(x):
+    members, regions = lax.axis_size("member"), lax.axis_size("region")
+    pairs = []
+    for a in range(members - 1):
+        pairs.append((a * regions + regions - 1, (a + 1) * regions + regions - 1))
+        pairs.append(((a + 1) * regions, a * regions))
+    return lax.ppermute(x, ("member", "region"), pairs)
+
+
 def local(ensemble, obs_value, obs_error, obs_index, obs_count):
     m = lax.axis_index("member").astype(jnp.int32)
     where = m.reshape(1)
-    tiled = ensemble.reshape(HELD, ROWS, GROUPS, 2, 8, 4, 128).transpose(2, 0, 1, 3, 5, 4, 6)
-    parts = []
-    for s in range(GROUPS):
-        to = m ^ s
-        part = lax.dynamic_index_in_dim(tiled, to, 0, keepdims=False)
-        edges = [
-            lax.dynamic_slice_in_dim(ensemble, jnp.clip(at, 0, GROUPS * COLS - 1), 1, 2)
-            for at in (to * COLS - 1, to * COLS + COLS)
-        ]
-        part = jnp.concatenate([x.reshape(-1, 128) for x in (part, *edges)], axis=0)
-        parts.append(swapped(part, s) if s else part)
-
+    tiled = ensemble.reshape(HELD, ROWS, 2 * GROUPS, 8, 4, 128).transpose(0, 1, 2, 4, 3, 5).reshape(-1, 128)
+    pieces = pl.pallas_call(
+        pack_kernel,
+        out_shape=[f32(PART_ROWS, 128)] * GROUPS,
+        in_specs=[pl.BlockSpec(memory_space=pltpu.SMEM), pl.BlockSpec(memory_space=pltpu.HBM)],
+        scratch_shapes=[
+            pltpu.VMEM((HELD * ROWS * GROUPS * 64, 128), jnp.float32),
+            pltpu.SemaphoreType.DMA((HELD * ROWS,)),
+        ],
+        compiler_params=pltpu.CompilerParams(vmem_limit_bytes=54000000),
+    )(where, tiled)
     slot = lax.broadcasted_iota(jnp.int32, (32, 1, OBS), 2)
     live = jnp.where(slot < obs_count[:, :, None], 1.0, 0.0).astype(jnp.float32)
     root_weight = jnp.sqrt(live / obs_error)
-    pieces = [obs_value, root_weight, obs_index.astype(jnp.float32), jnp.zeros_like(obs_value)]
-    packed = jnp.concatenate([x.reshape(COLS, ROWS, OBS) for x in pieces], axis=1)
+    columns = [obs_value, root_weight, obs_index.astype(jnp.float32), jnp.zeros_like(obs_value)]
+    packed = jnp.concatenate([x.reshape(COLS, ROWS, OBS) for x in columns], axis=1)
+    beside = edge_columns(packed)
+    packed = jnp.concatenate([packed, beside], axis=1)
+    parts = [swapped(pieces[s], s) if s else pieces[s] for s in range(GROUPS)]
+
     obs = lax.all_to_all(packed, "region", split_axis=0, concat_axis=0, tiled=True)
-
-    west = shifted(obs[COLS - 1], "member", 1)
-    east = shifted(obs[0], "member", -1)
 
     ens, slab0, slab1 = vmem_call(
         observe_kernel,
         (f32(MEMBERS * PITCH, 128), f32(SLAB_ROWS, OBS), f32(SLAB_ROWS, OBS)),
         10**9,
-        [where, *parts, obs, west, east],
+        [where, *parts, obs],
         [pltpu.VMEM((MEMBERS * EDGE_PITCH, 128), jnp.float32)],
     )
 

time: 103 us -> 85 us (0.83)
  the two profiles are of different devices: /device:TPU:33 before, /device:TPU:113 now
where the time goes in v2:
time: 85 us; the launch traced here: 84.8 us
  starting transfers between devices  29.6 us (35%)
  waiting for transfers between devices  26 us (31%)
  Pallas kernels  15.6 us (18%)
  blocking collectives  11.7 us (14%)
  local copies, waits for them, and re-layouts  1.54 us (2%)
    ppermute x14, waiting for transfers between devices, swapped(): return lax.ppermute(x, 'member', [(a, a ^ s) for a in range(GROUPS)])  22.7 us
    ppermute x14, starting transfers between devices, swapped(): return lax.ppermute(x, 'member', [(a, a ^ s) for a in range(GROUPS)])  20.3 us
    pallas_call x3, Pallas kernels, vmem_call(): pl.pallas_call(kernel, out_shape=out_shape, in_specs=places, scratch_shap...  14.1 us
    all_to_all x1, blocking collectives, local(): lax.all_to_all(packed, 'region', split_axis=0, concat_axis=0, tiled=True)  11.7 us
    ppermute x2, starting transfers between devices, shifted(): return lax.ppermute(x, axis, pairs)  8.58 us
    ppermute x2, waiting for transfers between devices, shifted(): return lax.ppermute(x, axis, pairs)  3.24 us
  transfers between devices with their start and end apart: 17, of which 8 were waited for; matrix products, arithmetic and copies ran while one was open for 1% of the time, Pallas kernels for 5%

profile of v2, /device:TPU:113, one launch (start us, length us, event | category | flops | bytes accessed | tf_op | source)
XLA Modules:
  0.0 84.8 jit_solution(14013410829165956068)
XLA Ops:
  0.0 0.0 copy-start.1
  0.0 1.5 %shard_map.58 = (f32[432,128]{1,0:T(8,128)S(1)}, f32[432,128]{1,0:T(8,128)S(1)}, f32[432,128]{1,0:T(8,128)S(1)}, f32[432,128]{1,0:T(8,128)S(1)}, f32[432,128]{1,...) custom-call(s32[1]{0:T(128)} %bitcast.m_ref, f32[3072,128]{1,0:T(8,128)} %bitcast.38), custom_call_target="tpu_custom_call" | custom-call | tf_op jit(solution)/shard_map/pallas_call | solution.py:384
  1.5 0.8 collective-permute-start
  2.2 1.2 %collective-permute-start.1 = (f32[432,128]{1,0:T(8,128)S(1)}, f32[432,128]{1,0:T(8,128)S(1)}, u32[]{:S(2)}, u32[]{:S(2)}) collective-permute-start(f32[432,128]{1,0:T(8,128)S(1)} %get-tuple-element.29), channel_id=1, source_target_pairs={{0,32},{16,48},{32,0},{48,16},{64,96},{80,112},{96,64},{112,80},{1... | collective-permute-start | bytes 663560 | tf_op jit(solution)/shard_map/ppermute | solution.py:362
  3.5 0.0 copy-done.4
  3.5 0.0 copy-done.2
  3.5 0.1 fusion.1
  3.6 0.0 copy-done.1
  3.7 0.7 collective-permute-start.7
  4.4 0.6 collective-permute-start.2
  4.9 2.7 %collective-permute-start.3 = (f32[432,128]{1,0:T(8,128)S(1)}, f32[432,128]{1,0:T(8,128)S(1)}, u32[]{:S(2)}, u32[]{:S(2)}) collective-permute-start(f32[432,128]{1,0:T(8,128)S(1)} %get-tuple-element.31), channel_id=1, source_target_pairs={{0,64},{16,80},{32,96},{48,112},{64,0},{80,16},{96,32},{112,48},{1... | collective-permute-start | bytes 663560 | tf_op jit(solution)/shard_map/ppermute | solution.py:362
  7.7 0.0 collective-permute-done.7
  7.7 0.5 collective-permute-start.4
  8.2 0.0 collective-permute-done.refs_1_
  8.2 2.5 %collective-permute-start.5 = (f32[432,128]{1,0:T(8,128)S(1)}, f32[432,128]{1,0:T(8,128)S(1)}, u32[]{:S(2)}, u32[]{:S(2)}) collective-permute-start(f32[432,128]{1,0:T(8,128)S(1)} %get-tuple-element.33), channel_id=1, source_target_pairs={{0,96},{16,112},{32,64},{48,80},{64,32},{80,48},{96,0},{112,16},{1... | collective-permute-start | bytes 663560 | tf_op jit(solution)/shard_map/ppermute | solution.py:362
  10.7 0.0 collective-permute-done.1.refs_2_
  10.7 2.3 %collective-permute-start.6 = (f32[432,128]{1,0:T(8,128)S(1)}, f32[432,128]{1,0:T(8,128)S(1)}, u32[]{:S(2)}, u32[]{:S(2)}) collective-permute-start(f32[432,128]{1,0:T(8,128)S(1)} %get-tuple-element.34), channel_id=1, source_target_pairs={{0,112},{16,96},{32,80},{48,64},{64,48},{80,32},{96,16},{112,0},{1... | collective-permute-start | bytes 663560 | tf_op jit(solution)/shard_map/ppermute | solution.py:362
  13.0 0.1 concatenate.8
  13.1 11.7 %all_to_all.5.refs_8_ = f32[16,16,128]{2,1,0:T(8,128)S(1)} all-to-all(f32[16,16,128]{2,1,0:T(8,128)S(1)} %concatenate.8), channel_id=1, replica_groups=mesh['member'=8,'region'=16] {'region'}, dimensions={0} | all-to-all | bytes 262144 | tf_op jit(solution)/shard_map/all_to_all | solution.py:403
  24.8 0.0 collective-permute-done.2.refs_3_
  24.8 0.0 collective-permute-done.3.refs_4_
  24.8 1.1 %collective-permute-done.4.refs_5_ = f32[432,128]{1,0:T(8,128)S(1)} collective-permute-done((f32[432,128]{1,0:T(8,128)S(1)}, f32[432,128]{1,0:T(8,128)S(1)}, u32[]{:S(2)}, u32[]{:S(2)}) %collective-permute-start.4) | collective-permute-done | bytes 221216 | tf_op jit(solution)/shard_map/ppermute | solution.py:362
  25.9 0.0 collective-permute-done.5.refs_6_
  25.9 4.9 %collective-permute-done.6.refs_7_ = f32[432,128]{1,0:T(8,128)S(1)} collective-permute-done((f32[432,128]{1,0:T(8,128)S(1)}, f32[432,128]{1,0:T(8,128)S(1)}, u32[]{:S(2)}, u32[]{:S(2)}) %collective-permute-start.6) | collective-permute-done | bytes 221216 | tf_op jit(solution)/shard_map/ppermute | solution.py:362
  30.8 1.6 %shard_map.59 = (f32[3168,128]{1,0:T(8,128)S(1)}, f32[472,128]{1,0:T(8,128)S(1)}, f32[472,128]{1,0:T(8,128)S(1)}) custom-call(s32[1]{0:T(128)} %bitcast.m_ref, f32[432,128]{1,0:T(8,128)S(1)} %get-tuple-element.27.refs_0_, f32[432,128]{1,0:T(8,128)S(1)} %collective-permute-done.refs_1_, f32[432,128]{1,0:T(8,128)S(1)} %collective-permute-done.1.refs_2_, ...), custom_call_target="tpu_custom_call" | custom-call | flops 1000000000 | tf_op jit(solution)/shard_map/pallas_call | solution.py:351
  32.4 6.7 %collective-permute-start.8 = (f32[472,128]{1,0:T(8,128)S(1)}, f32[472,128]{1,0:T(8,128)S(1)}, u32[]{:S(2)}, u32[]{:S(2)}) collective-permute-start(f32[472,128]{1,0:T(8,128)S(1)} %get-tuple-element.36.slab1_ref), channel_id=1, source_target_pairs={{0,1},{1,2},{2,3},{3,4},{4,5},{5,6},{6,7},{7,8},{8,9},{9,10},{10,1... | collective-permute-start | bytes 725000 | tf_op jit(solution)/shard_map/ppermute | solution.py:368
  39.1 1.9 %collective-permute-start.9 = (f32[472,128]{1,0:T(8,128)S(1)}, f32[472,128]{1,0:T(8,128)S(1)}, u32[]{:S(2)}, u32[]{:S(2)}) collective-permute-start(f32[472,128]{1,0:T(8,128)S(1)} %get-tuple-element.35.slab0_ref), channel_id=1, source_target_pairs={{1,0},{2,1},{3,2},{4,3},{5,4},{6,5},{7,6},{8,7},{9,8},{10,9},{11,1... | collective-permute-start | bytes 725000 | tf_op jit(solution)/shard_map/ppermute | solution.py:368
  41.0 4.1 %shard_map.60 = (f32[3584,128]{1,0:T(8,128)S(1)}, bf16[64,80,256]{2,1,0:T(8,128)(2,1)S(1)}, f32[128,128]{1,0:T(8,128)S(1)}) custom-call(f32[472,128]{1,0:T(8,128)S(1)} %get-tuple-element.35.slab0_ref, f32[472,128]{1,0:T(8,128)S(1)} %get-tuple-element.36.slab1_ref, f32[3168,128]{1,0:T(8,128)S(1)} %get-tuple-element.37.ens_ref), custom_call_target="tpu_custom_call" | custom-call | flops 4000000000 | tf_op jit(solution)/shard_map/pallas_call | solution.py:351
  45.1 0.0 collective-permute-done.8.above_ref
  45.1 3.2 %collective-permute-done.9.below_ref = f32[472,128]{1,0:T(8,128)S(1)} collective-permute-done((f32[472,128]{1,0:T(8,128)S(1)}, f32[472,128]{1,0:T(8,128)S(1)}, u32[]{:S(2)}, u32[]{:S(2)}) %collective-permute-start.9) | collective-permute-done | bytes 241696 | tf_op jit(solution)/shard_map/ppermute | solution.py:368
  48.3 8.5 %shard_map.61 = (f32[384,128]{1,0:T(8,128)S(1)}, f32[384,128]{1,0:T(8,128)S(1)}, f32[384,128]{1,0:T(8,128)S(1)}, f32[384,128]{1,0:T(8,128)S(1)}, f32[384,128]{1,...) custom-call(s32[1]{0:T(128)} %bitcast.m_ref, ...), custom_call_target="tpu_custom_call" | custom-call | flops 10000000000 | tf_op jit(solution)/shard_map/pallas_call | solution.py:351
  56.8 1.0 %collective-permute-start.10 = (f32[384,128]{1,0:T(8,128)S(1)}, f32[384,128]{1,0:T(8,128)S(1)}, u32[]{:S(2)}, u32[]{:S(2)}) collective-permute-start(f32[384,128]{1,0:T(8,128)S(1)} %get-tuple-element.42), channel_id=1, source_target_pairs={{0,16},{16,0},{32,48},{48,32},{64,80},{80,64},{96,112},{112,96},{1... | collective-permute-start | bytes 589832 | tf_op jit(solution)/shard_map/ppermute | solution.py:362
  57.8 0.0 collective-permute-start.11
  57.8 1.8 %collective-permute-start.12 = (f32[384,128]{1,0:T(8,128)S(1)}, f32[384,128]{1,0:T(8,128)S(1)}, u32[]{:S(2)}, u32[]{:S(2)}) collective-permute-start(f32[384,128]{1,0:T(8,128)S(1)} %get-tuple-element.44), channel_id=1, source_target_pairs={{0,48},{16,32},{32,16},{48,0},{64,112},{80,96},{96,80},{112,64},{1... | collective-permute-start | bytes 589832 | tf_op jit(solution)/shard_map/ppermute | solution.py:362
  59.6 0.7 collective-permute-start.13
  60.3 2.5 %collective-permute-start.14 = (f32[384,128]{1,0:T(8,128)S(1)}, f32[384,128]{1,0:T(8,128)S(1)}, u32[]{:S(2)}, u32[]{:S(2)}) collective-permute-start(f32[384,128]{1,0:T(8,128)S(1)} %get-tuple-element.46), channel_id=1, source_target_pairs={{0,80},{16,64},{32,112},{48,96},{64,16},{80,0},{96,48},{112,32},{1... | collective-permute-start | bytes 589832 | tf_op jit(solution)/shard_map/ppermute | solution.py:362
  62.8 0.2 broadcast_in_dim.12
  63.0 0.0 collective-permute-done.10
  63.1 1.3 %collective-permute-start.15 = (f32[384,128]{1,0:T(8,128)S(1)}, f32[384,128]{1,0:T(8,128)S(1)}, u32[]{:S(2)}, u32[]{:S(2)}) collective-permute-start(f32[384,128]{1,0:T(8,128)S(1)} %get-tuple-element.47), channel_id=1, source_target_pairs={{0,96},{16,112},{32,64},{48,80},{64,32},{80,48},{96,0},{112,16},{1... | collective-permute-start | bytes 589832 | tf_op jit(solution)/shard_map/ppermute | solution.py:362
  64.3 0.0 collective-permute-done.11
  64.3 2.5 %collective-permute-start.16 = (f32[384,128]{1,0:T(8,128)S(1)}, f32[384,128]{1,0:T(8,128)S(1)}, u32[]{:S(2)}, u32[]{:S(2)}) collective-permute-start(f32[384,128]{1,0:T(8,128)S(1)} %get-tuple-element.48), channel_id=1, source_target_pairs={{0,112},{16,96},{32,80},{48,64},{64,48},{80,32},{96,16},{112,0},{1... | collective-permute-start | bytes 589832 | tf_op jit(solution)/shard_map/ppermute | solution.py:362
  66.8 2.7 %collective-permute-done.12 = f32[384,128]{1,0:T(8,128)S(1)} collective-permute-done((f32[384,128]{1,0:T(8,128)S(1)}, f32[384,128]{1,0:T(8,128)S(1)}, u32[]{:S(2)}, u32[]{:S(2)}) %collective-permute-start.12) | collective-permute-done | bytes 196640 | tf_op jit(solution)/shard_map/ppermute | solution.py:362
  69.6 3.9 %collective-permute-done.13 = f32[384,128]{1,0:T(8,128)S(1)} collective-permute-done((f32[384,128]{1,0:T(8,128)S(1)}, f32[384,128]{1,0:T(8,128)S(1)}, u32[]{:S(2)}, u32[]{:S(2)}) %collective-permute-start.13) | collective-permute-done | bytes 196640 | tf_op jit(solution)/shard_map/ppermute | solution.py:362
  73.5 4.6 %collective-permute-done.14 = f32[384,128]{1,0:T(8,128)S(1)} collective-permute-done((f32[384,128]{1,0:T(8,128)S(1)}, f32[384,128]{1,0:T(8,128)S(1)}, u32[]{:S(2)}, u32[]{:S(2)}) %collective-permute-start.14) | collective-permute-done | bytes 196640 | tf_op jit(solution)/shard_map/ppermute | solution.py:362
  78.1 1.0 %collective-permute-done.15 = f32[384,128]{1,0:T(8,128)S(1)} collective-permute-done((f32[384,128]{1,0:T(8,128)S(1)}, f32[384,128]{1,0:T(8,128)S(1)}, u32[]{:S(2)}, u32[]{:S(2)}) %collective-permute-start.15) | collective-permute-done | bytes 196640 | tf_op jit(solution)/shard_map/ppermute | solution.py:362
  79.1 4.5 %collective-permute-done.16 = f32[384,128]{1,0:T(8,128)S(1)} collective-permute-done((f32[384,128]{1,0:T(8,128)S(1)}, f32[384,128]{1,0:T(8,128)S(1)}, u32[]{:S(2)}, u32[]{:S(2)}) %collective-permute-start.16) | collective-permute-done | bytes 196640 | tf_op jit(solution)/shard_map/ppermute | solution.py:362
  83.6 0.0 copy-start
  83.6 1.1 %copy-done = f32[3,2,8,2,4,8,128]{6,5,4,3,2,1,0:T(8,128)} copy-done((f32[3,2,8,2,4,8,128]{6,5,4,3,2,1,0:T(8,128)}, f32[3,2,8,2,4,8,128]{6,5,4,3,2,1,0:T(8,128)S(1)}, u32[]{:S(2)}) %copy-start) | copy-done | bytes 1572888
  (15 shorter events, 0.2 us)
Async XLA Ops:
  0.0 3.5 %copy-start.4 = (s32[32,1]{0,1:T(1,128)S(1)}, s32[32,1]{0,1:T(1,128)}, u32[]{:S(2)}) copy-start(s32[32,1]{0,1:T(1,128)} %param.9) | copy-start | bytes 388
  0.0 3.5 %copy-start.2 = (f32[32,1,128]{2,1,0:T(1,128)S(1)}, f32[32,1,128]{2,1,0:T(1,128)}, u32[]{:S(2)}) copy-start(f32[32,1,128]{2,1,0:T(1,128)} %param.7) | copy-start | bytes 49156
  0.0 3.6 %copy-start.3 = (s32[32,1,128]{2,1,0:T(1,128)S(1)}, s32[32,1,128]{2,1,0:T(1,128)}, u32[]{:S(2)}) copy-start(s32[32,1,128]{2,1,0:T(1,128)} %param.8) | copy-start | bytes 49156
  0.0 3.6 %copy-start.1 = (f32[32,1,128]{2,1,0:T(1,128)S(1)}, f32[32,1,128]{2,1,0:T(1,128)}, u32[]{:S(2)}) copy-start(f32[32,1,128]{2,1,0:T(1,128)} %param.6) | copy-start | bytes 49156
  1.5 6.7 %collective-permute-start = (f32[432,128]{1,0:T(8,128)S(1)}, f32[432,128]{1,0:T(8,128)S(1)}, u32[]{:S(2)}, u32[]{:S(2)}) collective-permute-start(f32[432,128]{1,0:T(8,128)S(1)} %get-tuple-element.28), channel_id=1, source_target_pairs={{0,16},{16,0},{32,48},{48,32},{64,80},{80,64},{96,112},{112,96},{1... | collective-permute-start | bytes 663560 | tf_op jit(solution)/shard_map/ppermute | solution.py:362
  2.2 8.5 %collective-permute-start.1 = (f32[432,128]{1,0:T(8,128)S(1)}, f32[432,128]{1,0:T(8,128)S(1)}, u32[]{:S(2)}, u32[]{:S(2)}) collective-permute-start(f32[432,128]{1,0:T(8,128)S(1)} %get-tuple-element.29), channel_id=1, source_target_pairs={{0,32},{16,48},{32,0},{48,16},{64,96},{80,112},{96,64},{112,80},{1... | collective-permute-start | bytes 663560 | tf_op jit(solution)/shard_map/ppermute | solution.py:362
  3.7 4.0 %collective-permute-start.7 = (f32[16,8,128]{2,1,0:T(8,128)S(1)}, f32[16,8,128]{2,1,0:T(8,128)S(1)}, u32[]{:S(2)}, u32[]{:S(2)}) collective-permute-start(f32[16,8,128]{2,1,0:T(8,128)S(1)} %pad_maximum_fusion), channel_id=1, source_target_pairs={{15,31},{16,0},{31,47},{32,16},{47,63},{48,32},{63,79},{64,48},{79... | collective-permute-start | bytes 196616 | tf_op jit(solution)/shard_map/ppermute | solution.py:377
  4.4 20.4 %collective-permute-start.2 = (f32[432,128]{1,0:T(8,128)S(1)}, f32[432,128]{1,0:T(8,128)S(1)}, u32[]{:S(2)}, u32[]{:S(2)}) collective-permute-start(f32[432,128]{1,0:T(8,128)S(1)} %get-tuple-element.30), channel_id=1, source_target_pairs={{0,48},{16,32},{32,16},{48,0},{64,112},{80,96},{96,80},{112,64},{1... | collective-permute-start | bytes 663560 | tf_op jit(solution)/shard_map/ppermute | solution.py:362
  4.9 19.9 %collective-permute-start.3 = (f32[432,128]{1,0:T(8,128)S(1)}, f32[432,128]{1,0:T(8,128)S(1)}, u32[]{:S(2)}, u32[]{:S(2)}) collective-permute-start(f32[432,128]{1,0:T(8,128)S(1)} %get-tuple-element.31), channel_id=1, source_target_pairs={{0,64},{16,80},{32,96},{48,112},{64,0},{80,16},{96,32},{112,48},{1... | collective-permute-start | bytes 663560 | tf_op jit(solution)/shard_map/ppermute | solution.py:362
  7.7 18.2 %collective-permute-start.4 = (f32[432,128]{1,0:T(8,128)S(1)}, f32[432,128]{1,0:T(8,128)S(1)}, u32[]{:S(2)}, u32[]{:S(2)}) collective-permute-start(f32[432,128]{1,0:T(8,128)S(1)} %get-tuple-element.32), channel_id=1, source_target_pairs={{0,80},{16,64},{32,112},{48,96},{64,16},{80,0},{96,48},{112,32},{1... | collective-permute-start | bytes 663560 | tf_op jit(solution)/shard_map/ppermute | solution.py:362
  8.2 17.7 %collective-permute-start.5 = (f32[432,128]{1,0:T(8,128)S(1)}, f32[432,128]{1,0:T(8,128)S(1)}, u32[]{:S(2)}, u32[]{:S(2)}) collective-permute-start(f32[432,128]{1,0:T(8,128)S(1)} %get-tuple-element.33), channel_id=1, source_target_pairs={{0,96},{16,112},{32,64},{48,80},{64,32},{80,48},{96,0},{112,16},{1... | collective-permute-start | bytes 663560 | tf_op jit(solution)/shard_map/ppermute | solution.py:362
  10.7 20.1 %collective-permute-start.6 = (f32[432,128]{1,0:T(8,128)S(1)}, f32[432,128]{1,0:T(8,128)S(1)}, u32[]{:S(2)}, u32[]{:S(2)}) collective-permute-start(f32[432,128]{1,0:T(8,128)S(1)} %get-tuple-element.34), channel_id=1, source_target_pairs={{0,112},{16,96},{32,80},{48,64},{64,48},{80,32},{96,16},{112,0},{1... | collective-permute-start | bytes 663560 | tf_op jit(solution)/shard_map/ppermute | solution.py:362
  32.4 12.7 %collective-permute-start.8 = (f32[472,128]{1,0:T(8,128)S(1)}, f32[472,128]{1,0:T(8,128)S(1)}, u32[]{:S(2)}, u32[]{:S(2)}) collective-permute-start(f32[472,128]{1,0:T(8,128)S(1)} %get-tuple-element.36.slab1_ref), channel_id=1, source_target_pairs={{0,1},{1,2},{2,3},{3,4},{4,5},{5,6},{6,7},{7,8},{8,9},{9,10},{10,1... | collective-permute-start | bytes 725000 | tf_op jit(solution)/shard_map/ppermute | solution.py:368
  39.1 9.2 %collective-permute-start.9 = (f32[472,128]{1,0:T(8,128)S(1)}, f32[472,128]{1,0:T(8,128)S(1)}, u32[]{:S(2)}, u32[]{:S(2)}) collective-permute-start(f32[472,128]{1,0:T(8,128)S(1)} %get-tuple-element.35.slab0_ref), channel_id=1, source_target_pairs={{1,0},{2,1},{3,2},{4,3},{5,4},{6,5},{7,6},{8,7},{9,8},{10,9},{11,1... | collective-permute-start | bytes 725000 | tf_op jit(solution)/shard_map/ppermute | solution.py:368
  56.8 6.2 %collective-permute-start.10 = (f32[384,128]{1,0:T(8,128)S(1)}, f32[384,128]{1,0:T(8,128)S(1)}, u32[]{:S(2)}, u32[]{:S(2)}) collective-permute-start(f32[384,128]{1,0:T(8,128)S(1)} %get-tuple-element.42), channel_id=1, source_target_pairs={{0,16},{16,0},{32,48},{48,32},{64,80},{80,64},{96,112},{112,96},{1... | collective-permute-start | bytes 589832 | tf_op jit(solution)/shard_map/ppermute | solution.py:362
  57.8 6.5 %collective-permute-start.11 = (f32[384,128]{1,0:T(8,128)S(1)}, f32[384,128]{1,0:T(8,128)S(1)}, u32[]{:S(2)}, u32[]{:S(2)}) collective-permute-start(f32[384,128]{1,0:T(8,128)S(1)} %get-tuple-element.43), channel_id=1, source_target_pairs={{0,32},{16,48},{32,0},{48,16},{64,96},{80,112},{96,64},{112,80},{1... | collective-permute-start | bytes 589832 | tf_op jit(solution)/shard_map/ppermute | solution.py:362
  57.8 11.7 %collective-permute-start.12 = (f32[384,128]{1,0:T(8,128)S(1)}, f32[384,128]{1,0:T(8,128)S(1)}, u32[]{:S(2)}, u32[]{:S(2)}) collective-permute-start(f32[384,128]{1,0:T(8,128)S(1)} %get-tuple-element.44), channel_id=1, source_target_pairs={{0,48},{16,32},{32,16},{48,0},{64,112},{80,96},{96,80},{112,64},{1... | collective-permute-start | bytes 589832 | tf_op jit(solution)/shard_map/ppermute | solution.py:362
  59.6 13.9 %collective-permute-start.13 = (f32[384,128]{1,0:T(8,128)S(1)}, f32[384,128]{1,0:T(8,128)S(1)}, u32[]{:S(2)}, u32[]{:S(2)}) collective-permute-start(f32[384,128]{1,0:T(8,128)S(1)} %get-tuple-element.45), channel_id=1, source_target_pairs={{0,64},{16,80},{32,96},{48,112},{64,0},{80,16},{96,32},{112,48},{1... | collective-permute-start | bytes 589832 | tf_op jit(solution)/shard_map/ppermute | solution.py:362
  60.3 17.8 %collective-permute-start.14 = (f32[384,128]{1,0:T(8,128)S(1)}, f32[384,128]{1,0:T(8,128)S(1)}, u32[]{:S(2)}, u32[]{:S(2)}) collective-permute-start(f32[384,128]{1,0:T(8,128)S(1)} %get-tuple-element.46), channel_id=1, source_target_pairs={{0,80},{16,64},{32,112},{48,96},{64,16},{80,0},{96,48},{112,32},{1... | collective-permute-start | bytes 589832 | tf_op jit(solution)/shard_map/ppermute | solution.py:362
  63.1 16.0 %collective-permute-start.15 = (f32[384,128]{1,0:T(8,128)S(1)}, f32[384,128]{1,0:T(8,128)S(1)}, u32[]{:S(2)}, u32[]{:S(2)}) collective-permute-start(f32[384,128]{1,0:T(8,128)S(1)} %get-tuple-element.47), channel_id=1, source_target_pairs={{0,96},{16,112},{32,64},{48,80},{64,32},{80,48},{96,0},{112,16},{1... | collective-permute-start | bytes 589832 | tf_op jit(solution)/shard_map/ppermute | solution.py:362
  64.3 19.3 %collective-permute-start.16 = (f32[384,128]{1,0:T(8,128)S(1)}, f32[384,128]{1,0:T(8,128)S(1)}, u32[]{:S(2)}, u32[]{:S(2)}) collective-permute-start(f32[384,128]{1,0:T(8,128)S(1)} %get-tuple-element.48), channel_id=1, source_target_pairs={{0,112},{16,96},{32,80},{48,64},{64,48},{80,32},{96,16},{112,0},{1... | collective-permute-start | bytes 589832 | tf_op jit(solution)/shard_map/ppermute | solution.py:362
  83.6 1.1 %copy-start = (f32[3,2,8,2,4,8,128]{6,5,4,3,2,1,0:T(8,128)}, f32[3,2,8,2,4,8,128]{6,5,4,3,2,1,0:T(8,128)S(1)}, u32[]{:S(2)}) copy-start(f32[3,2,8,2,4,8,128]{6,5,4,3,2,1,0:T(8,128)S(1)} %constant_dynamic-update-slice_fusion) | copy-start | bytes 4718596

commit v3 on v2

--- a/solution.py
+++ b/solution.py
@@ -362,10 +362,12 @@
     return lax.ppermute(x, "member", [(a, a ^ s) for a in range(GROUPS)])
 
 
-def shifted(x, axis, by):
-    devices = lax.axis_size(axis)
-    pairs = [(i, i + by) for i in range(devices) if 0 <= i + by < devices]
-    return lax.ppermute(x, axis, pairs)
+def paired(x, start):
+    regions = lax.axis_size("region")
+    pairs = []
+    for a in range(start, regions - 1, 2):
+        pairs += [(a, a + 1), (a + 1, a)]
+    return lax.ppermute(x, "region", pairs)
 
 
 def edge_columns(x):
@@ -410,8 +412,11 @@
         [pltpu.VMEM((MEMBERS * EDGE_PITCH, 128), jnp.float32)],
     )
 
-    below = shifted(slab0, "region", -1)
-    above = shifted(slab1, "region", 1)
+    odd = (lax.axis_index("region") & 1) == 1
+    first = paired(jnp.where(odd, slab0, slab1), 0)
+    second = paired(jnp.where(odd, slab1, slab0), 1)
+    above = jnp.where(odd, first, second)
+    below = jnp.where(odd, second, first)
 
     own, stack, mean = vmem_call(
         own_gram_kernel,

time: 85 us -> 83.2 us (0.979)
  blocking collectives: 11.7 us -> 0 us
  starting transfers between devices: 29.6 us -> 36.2 us
  waiting for transfers between devices: 26 us -> 28 us
  local copies, waits for them, and re-layouts: 1.54 us -> 2.79 us
    all_to_all x1 -> x0, blocking collectives: 11.7 us -> none  [local(): lax.all_to_all(packed, 'region', split_axis=0, concat_axis=0, tiled=True)]
    all_to_all x0 -> x1, starting transfers between devices: none -> 8.44 us  [local(): lax.all_to_all(packed, 'region', split_axis=0, concat_axis=0, tiled=True)]
    all_to_all x0 -> x1, waiting for transfers between devices: none -> 3.5 us  [local(): lax.all_to_all(packed, 'region', split_axis=0, concat_axis=0, tiled=True)]
    ppermute x2, starting transfers between devices: 8.58 us -> 6.74 us  [paired(): return lax.ppermute(x, 'region', pairs)]
    ppermute x14, waiting for transfers between devices: 22.7 us -> 21.3 us  [swapped(): return lax.ppermute(x, 'member', [(a, a ^ s) for a in range(GROUPS)])]
    concatenate x1, local copies, waits for them, and re-layouts: 0.06 us -> 1.31 us  [local(): packed = jnp.concatenate([packed, beside], axis=1)]
  transfers between devices with their start and end apart: 17 -> 18, of which waited for: 8 -> 9; matrix products, arithmetic and copies ran while one was open for 1% -> 2% of each run, Pallas kernels for 5% -> 5%
where the time goes in v3:
time: 83.2 us; the launch traced here: 83 us
  starting transfers between devices  36.2 us (44%)
  waiting for transfers between devices  28 us (34%)
  Pallas kernels  15.5 us (19%)
  local copies, waits for them, and re-layouts  2.79 us (3%)
    ppermute x14, waiting for transfers between devices, swapped(): return lax.ppermute(x, 'member', [(a, a ^ s) for a in range(GROUPS)])  21.3 us
    ppermute x14, starting transfers between devices, swapped(): return lax.ppermute(x, 'member', [(a, a ^ s) for a in range(GROUPS)])  20.3 us
    pallas_call x3, Pallas kernels, vmem_call(): pl.pallas_call(kernel, out_shape=out_shape, in_specs=places, scratch_shap...  14.1 us
    all_to_all x1, starting transfers between devices, local(): lax.all_to_all(packed, 'region', split_axis=0, concat_axis=0, tiled=True)  8.44 us
    ppermute x2, starting transfers between devices, paired(): return lax.ppermute(x, 'region', pairs)  6.74 us
    all_to_all x1, waiting for transfers between devices, local(): lax.all_to_all(packed, 'region', split_axis=0, concat_axis=0, tiled=True)  3.5 us
    ppermute x2, waiting for transfers between devices, paired(): return lax.ppermute(x, 'region', pairs)  3.25 us
  transfers between devices with their start and end apart: 18, of which 9 were waited for; matrix products, arithmetic and copies ran while one was open for 2% of the time, Pallas kernels for 5%

profile of v3, /device:TPU:113, one launch (start us, length us, event | category | flops | bytes accessed | tf_op | source)
XLA Modules:
  0.0 83.0 jit_solution(11766532594974276069)
XLA Ops:
  0.0 0.0 copy-start.1
  0.0 1.5 %shard_map.58 = (f32[432,128]{1,0:T(8,128)S(1)}, f32[432,128]{1,0:T(8,128)S(1)}, f32[432,128]{1,0:T(8,128)S(1)}, f32[432,128]{1,0:T(8,128)S(1)}, f32[432,128]{1,...) custom-call(s32[1]{0:T(128)} %bitcast.m_ref, f32[3072,128]{1,0:T(8,128)} %bitcast.38), custom_call_target="tpu_custom_call" | custom-call | tf_op jit(solution)/shard_map/pallas_call | solution.py:386
  1.5 0.8 collective-permute-start
  2.2 1.2 %collective-permute-start.1 = (f32[432,128]{1,0:T(8,128)S(1)}, f32[432,128]{1,0:T(8,128)S(1)}, u32[]{:S(2)}, u32[]{:S(2)}) collective-permute-start(f32[432,128]{1,0:T(8,128)S(1)} %get-tuple-element.29), channel_id=1, source_target_pairs={{0,32},{16,48},{32,0},{48,16},{64,96},{80,112},{96,64},{112,80},{1... | collective-permute-start | bytes 663560 | tf_op jit(solution)/shard_map/ppermute | solution.py:362
  3.5 0.0 copy-done.2
  3.5 0.1 fusion.1
  3.7 0.7 collective-permute-start.7
  4.4 0.6 collective-permute-start.2
  4.9 2.7 %collective-permute-start.3 = (f32[432,128]{1,0:T(8,128)S(1)}, f32[432,128]{1,0:T(8,128)S(1)}, u32[]{:S(2)}, u32[]{:S(2)}) collective-permute-start(f32[432,128]{1,0:T(8,128)S(1)} %get-tuple-element.31), channel_id=1, source_target_pairs={{0,64},{16,80},{32,96},{48,112},{64,0},{80,16},{96,32},{112,48},{1... | collective-permute-start | bytes 663560 | tf_op jit(solution)/shard_map/ppermute | solution.py:362
  7.7 0.0 collective-permute-done.7
  7.7 0.5 collective-permute-start.4
  8.2 0.0 collective-permute-done.refs_1_
  8.2 2.5 %collective-permute-start.5 = (f32[432,128]{1,0:T(8,128)S(1)}, f32[432,128]{1,0:T(8,128)S(1)}, u32[]{:S(2)}, u32[]{:S(2)}) collective-permute-start(f32[432,128]{1,0:T(8,128)S(1)} %get-tuple-element.33), channel_id=1, source_target_pairs={{0,96},{16,112},{32,64},{48,80},{64,32},{80,48},{96,0},{112,16},{1... | collective-permute-start | bytes 663560 | tf_op jit(solution)/shard_map/ppermute | solution.py:362
  10.7 0.0 collective-permute-done.1.refs_2_
  10.7 2.3 %collective-permute-start.6 = (f32[432,128]{1,0:T(8,128)S(1)}, f32[432,128]{1,0:T(8,128)S(1)}, u32[]{:S(2)}, u32[]{:S(2)}) collective-permute-start(f32[432,128]{1,0:T(8,128)S(1)} %get-tuple-element.34), channel_id=1, source_target_pairs={{0,112},{16,96},{32,80},{48,64},{64,48},{80,32},{96,16},{112,0},{1... | collective-permute-start | bytes 663560 | tf_op jit(solution)/shard_map/ppermute | solution.py:362
  13.0 1.3 %concatenate.8 = f32[16,16,128]{2,1,0:T(8,128)} concatenate(f32[16,2,128]{2,1,0:T(2,128)S(1)} %bitcast.51, f32[16,2,128]{2,1,0:T(2,128)S(1)} %bitcast.47, f32[16,2,128]{2,1,0:T(2,128)S(1)} %bitcast.49, f32[16,2,128]{2,1,0:T(2,128)S(1)} %reshape.93, f32[16,8,128]{2,1,0:T(8,128)S(1)} %collective-permute-done.7), dimensions={1} | concatenate | bytes 262144 | tf_op jit(solution)/shard_map/concatenate | solution.py:402
  14.3 8.4 %all-to-all-start = ((f32[16,16,128]{2,1,0:T(8,128)}), f32[16,16,128]{2,1,0:T(8,128)S(1)}, u32[]{:S(2)}, u32[]{:S(2)}) async-start(f32[16,16,128]{2,1,0:T(8,128)} %concatenate.8), calls=%async_computation | async-start | bytes 262144 | tf_op jit(solution)/shard_map/all_to_all | solution.py:405
  22.8 3.5 %all-to-all-done.refs_8_ = f32[16,16,128]{2,1,0:T(8,128)S(1)} async-done(((f32[16,16,128]{2,1,0:T(8,128)}), f32[16,16,128]{2,1,0:T(8,128)S(1)}, u32[]{:S(2)}, u32[]{:S(2)}) %all-to-all-start) | async-done | bytes 131104 | tf_op jit(solution)/shard_map/all_to_all | solution.py:405
  26.3 0.0 collective-permute-done.2.refs_3_
  26.3 0.0 collective-permute-done.3.refs_4_
  26.3 0.0 collective-permute-done.4.refs_5_
  26.3 0.0 collective-permute-done.5.refs_6_
  26.3 4.5 %collective-permute-done.6.refs_7_ = f32[432,128]{1,0:T(8,128)S(1)} collective-permute-done((f32[432,128]{1,0:T(8,128)S(1)}, f32[432,128]{1,0:T(8,128)S(1)}, u32[]{:S(2)}, u32[]{:S(2)}) %collective-permute-start.6) | collective-permute-done | bytes 221216 | tf_op jit(solution)/shard_map/ppermute | solution.py:362
  30.8 1.6 %shard_map.59 = (f32[3168,128]{1,0:T(8,128)S(1)}, f32[472,128]{1,0:T(8,128)S(1)}, f32[472,128]{1,0:T(8,128)S(1)}) custom-call(s32[1]{0:T(128)} %bitcast.m_ref, f32[432,128]{1,0:T(8,128)S(1)} %get-tuple-element.27.refs_0_, f32[432,128]{1,0:T(8,128)S(1)} %collective-permute-done.refs_1_, f32[432,128]{1,0:T(8,128)S(1)} %collective-permute-done.1.refs_2_, ...), custom_call_target="tpu_custom_call" | custom-call | flops 1000000000 | tf_op jit(solution)/shard_map/pallas_call | solution.py:351
  32.4 0.1 broadcast_select_fusion.2
  32.5 4.8 %collective-permute-start.8 = (f32[472,128]{1,0:T(8,128)S(1)}, f32[472,128]{1,0:T(8,128)S(1)}, u32[]{:S(2)}, u32[]{:S(2)}) collective-permute-start(f32[472,128]{1,0:T(8,128)S(1)} %get-tuple-element.52), channel_id=1, source_target_pairs={{0,1},{1,0},{2,3},{3,2},{4,5},{5,4},{6,7},{7,6},{8,9},{9,8},{10,11... | collective-permute-start | bytes 725000 | tf_op jit(solution)/shard_map/ppermute | solution.py:370
  37.3 1.9 %collective-permute-start.9 = (f32[472,128]{1,0:T(8,128)S(1)}, f32[472,128]{1,0:T(8,128)S(1)}, u32[]{:S(2)}, u32[]{:S(2)}) collective-permute-start(f32[472,128]{1,0:T(8,128)S(1)} %get-tuple-element.51), channel_id=1, source_target_pairs={{1,2},{2,1},{3,4},{4,3},{5,6},{6,5},{7,8},{8,7},{9,10},{10,9},{11,... | collective-permute-start | bytes 725000 | tf_op jit(solution)/shard_map/ppermute | solution.py:370
  39.2 4.0 %shard_map.60 = (f32[3584,128]{1,0:T(8,128)S(1)}, bf16[64,80,256]{2,1,0:T(8,128)(2,1)S(1)}, f32[128,128]{1,0:T(8,128)S(1)}) custom-call(f32[472,128]{1,0:T(8,128)S(1)} %get-tuple-element.35.slab0_ref, f32[472,128]{1,0:T(8,128)S(1)} %get-tuple-element.36.slab1_ref, f32[3168,128]{1,0:T(8,128)S(1)} %get-tuple-element.37.ens_ref), custom_call_target="tpu_custom_call" | custom-call | flops 4000000000 | tf_op jit(solution)/shard_map/pallas_call | solution.py:351
  43.3 0.4 collective-permute-done.8
  43.7 2.8 %collective-permute-done.9 = f32[472,128]{1,0:T(8,128)S(1)} collective-permute-done((f32[472,128]{1,0:T(8,128)S(1)}, f32[472,128]{1,0:T(8,128)S(1)}, u32[]{:S(2)}, u32[]{:S(2)}) %collective-permute-start.9) | collective-permute-done | bytes 241696 | tf_op jit(solution)/shard_map/ppermute | solution.py:370
  46.6 8.4 %shard_map.61 = (f32[384,128]{1,0:T(8,128)S(1)}, f32[384,128]{1,0:T(8,128)S(1)}, f32[384,128]{1,0:T(8,128)S(1)}, f32[384,128]{1,0:T(8,128)S(1)}, f32[384,128]{1,...) custom-call(s32[1]{0:T(128)} %bitcast.m_ref, ...), custom_call_target="tpu_custom_call" | custom-call | flops 10000000000 | tf_op jit(solution)/shard_map/pallas_call | solution.py:351
  55.0 1.0 %collective-permute-start.10 = (f32[384,128]{1,0:T(8,128)S(1)}, f32[384,128]{1,0:T(8,128)S(1)}, u32[]{:S(2)}, u32[]{:S(2)}) collective-permute-start(f32[384,128]{1,0:T(8,128)S(1)} %get-tuple-element.42), channel_id=1, source_target_pairs={{0,16},{16,0},{32,48},{48,32},{64,80},{80,64},{96,112},{112,96},{1... | collective-permute-start | bytes 589832 | tf_op jit(solution)/shard_map/ppermute | solution.py:362
  56.0 0.0 collective-permute-start.11
  56.0 1.8 %collective-permute-start.12 = (f32[384,128]{1,0:T(8,128)S(1)}, f32[384,128]{1,0:T(8,128)S(1)}, u32[]{:S(2)}, u32[]{:S(2)}) collective-permute-start(f32[384,128]{1,0:T(8,128)S(1)} %get-tuple-element.44), channel_id=1, source_target_pairs={{0,48},{16,32},{32,16},{48,0},{64,112},{80,96},{96,80},{112,64},{1... | collective-permute-start | bytes 589832 | tf_op jit(solution)/shard_map/ppermute | solution.py:362
  57.8 0.7 collective-permute-start.13
  58.5 2.5 %collective-permute-start.14 = (f32[384,128]{1,0:T(8,128)S(1)}, f32[384,128]{1,0:T(8,128)S(1)}, u32[]{:S(2)}, u32[]{:S(2)}) collective-permute-start(f32[384,128]{1,0:T(8,128)S(1)} %get-tuple-element.46), channel_id=1, source_target_pairs={{0,80},{16,64},{32,112},{48,96},{64,16},{80,0},{96,48},{112,32},{1... | collective-permute-start | bytes 589832 | tf_op jit(solution)/shard_map/ppermute | solution.py:362
  61.0 0.2 broadcast_in_dim.12
  61.3 0.0 collective-permute-done.10
  61.3 1.3 %collective-permute-start.15 = (f32[384,128]{1,0:T(8,128)S(1)}, f32[384,128]{1,0:T(8,128)S(1)}, u32[]{:S(2)}, u32[]{:S(2)}) collective-permute-start(f32[384,128]{1,0:T(8,128)S(1)} %get-tuple-element.47), channel_id=1, source_target_pairs={{0,96},{16,112},{32,64},{48,80},{64,32},{80,48},{96,0},{112,16},{1... | collective-permute-start | bytes 589832 | tf_op jit(solution)/shard_map/ppermute | solution.py:362
  62.5 0.0 collective-permute-done.11
  62.5 2.5 %collective-permute-start.16 = (f32[384,128]{1,0:T(8,128)S(1)}, f32[384,128]{1,0:T(8,128)S(1)}, u32[]{:S(2)}, u32[]{:S(2)}) collective-permute-start(f32[384,128]{1,0:T(8,128)S(1)} %get-tuple-element.48), channel_id=1, source_target_pairs={{0,112},{16,96},{32,80},{48,64},{64,48},{80,32},{96,16},{112,0},{1... | collective-permute-start | bytes 589832 | tf_op jit(solution)/shard_map/ppermute | solution.py:362
  65.0 2.7 %collective-permute-done.12 = f32[384,128]{1,0:T(8,128)S(1)} collective-permute-done((f32[384,128]{1,0:T(8,128)S(1)}, f32[384,128]{1,0:T(8,128)S(1)}, u32[]{:S(2)}, u32[]{:S(2)}) %collective-permute-start.12) | collective-permute-done | bytes 196640 | tf_op jit(solution)/shard_map/ppermute | solution.py:362
  67.8 3.9 %collective-permute-done.13 = f32[384,128]{1,0:T(8,128)S(1)} collective-permute-done((f32[384,128]{1,0:T(8,128)S(1)}, f32[384,128]{1,0:T(8,128)S(1)}, u32[]{:S(2)}, u32[]{:S(2)}) %collective-permute-start.13) | collective-permute-done | bytes 196640 | tf_op jit(solution)/shard_map/ppermute | solution.py:362
  71.7 4.6 %collective-permute-done.14 = f32[384,128]{1,0:T(8,128)S(1)} collective-permute-done((f32[384,128]{1,0:T(8,128)S(1)}, f32[384,128]{1,0:T(8,128)S(1)}, u32[]{:S(2)}, u32[]{:S(2)}) %collective-permute-start.14) | collective-permute-done | bytes 196640 | tf_op jit(solution)/shard_map/ppermute | solution.py:362
  76.3 1.0 %collective-permute-done.15 = f32[384,128]{1,0:T(8,128)S(1)} collective-permute-done((f32[384,128]{1,0:T(8,128)S(1)}, f32[384,128]{1,0:T(8,128)S(1)}, u32[]{:S(2)}, u32[]{:S(2)}) %collective-permute-start.15) | collective-permute-done | bytes 196640 | tf_op jit(solution)/shard_map/ppermute | solution.py:362
  77.3 4.5 %collective-permute-done.16 = f32[384,128]{1,0:T(8,128)S(1)} collective-permute-done((f32[384,128]{1,0:T(8,128)S(1)}, f32[384,128]{1,0:T(8,128)S(1)}, u32[]{:S(2)}, u32[]{:S(2)}) %collective-permute-start.16) | collective-permute-done | bytes 196640 | tf_op jit(solution)/shard_map/ppermute | solution.py:362
  81.8 0.0 copy-start
  81.9 1.1 %copy-done = f32[3,2,8,2,4,8,128]{6,5,4,3,2,1,0:T(8,128)} copy-done((f32[3,2,8,2,4,8,128]{6,5,4,3,2,1,0:T(8,128)}, f32[3,2,8,2,4,8,128]{6,5,4,3,2,1,0:T(8,128)S(1)}, u32[]{:S(2)}) %copy-start) | copy-done | bytes 1572888
  (18 shorter events, 0.2 us)
Async XLA Ops:
  0.0 3.5 %copy-start.4 = (s32[32,1]{0,1:T(1,128)S(1)}, s32[32,1]{0,1:T(1,128)}, u32[]{:S(2)}) copy-start(s32[32,1]{0,1:T(1,128)} %param.9) | copy-start | bytes 388
  0.0 3.5 %copy-start.2 = (f32[32,1,128]{2,1,0:T(1,128)S(1)}, f32[32,1,128]{2,1,0:T(1,128)}, u32[]{:S(2)}) copy-start(f32[32,1,128]{2,1,0:T(1,128)} %param.7) | copy-start | bytes 49156
  0.0 3.6 %copy-start.3 = (s32[32,1,128]{2,1,0:T(1,128)S(1)}, s32[32,1,128]{2,1,0:T(1,128)}, u32[]{:S(2)}) copy-start(s32[32,1,128]{2,1,0:T(1,128)} %param.8) | copy-start | bytes 49156
  0.0 3.6 %copy-start.1 = (f32[32,1,128]{2,1,0:T(1,128)S(1)}, f32[32,1,128]{2,1,0:T(1,128)}, u32[]{:S(2)}) copy-start(f32[32,1,128]{2,1,0:T(1,128)} %param.6) | copy-start | bytes 49156
  1.5 6.7 %collective-permute-start = (f32[432,128]{1,0:T(8,128)S(1)}, f32[432,128]{1,0:T(8,128)S(1)}, u32[]{:S(2)}, u32[]{:S(2)}) collective-permute-start(f32[432,128]{1,0:T(8,128)S(1)} %get-tuple-element.28), channel_id=1, source_target_pairs={{0,16},{16,0},{32,48},{48,32},{64,80},{80,64},{96,112},{112,96},{1... | collective-permute-start | bytes 663560 | tf_op jit(solution)/shard_map/ppermute | solution.py:362
  2.2 8.5 %collective-permute-start.1 = (f32[432,128]{1,0:T(8,128)S(1)}, f32[432,128]{1,0:T(8,128)S(1)}, u32[]{:S(2)}, u32[]{:S(2)}) collective-permute-start(f32[432,128]{1,0:T(8,128)S(1)} %get-tuple-element.29), channel_id=1, source_target_pairs={{0,32},{16,48},{32,0},{48,16},{64,96},{80,112},{96,64},{112,80},{1... | collective-permute-start | bytes 663560 | tf_op jit(solution)/shard_map/ppermute | solution.py:362
  3.7 4.0 %collective-permute-start.7 = (f32[16,8,128]{2,1,0:T(8,128)S(1)}, f32[16,8,128]{2,1,0:T(8,128)S(1)}, u32[]{:S(2)}, u32[]{:S(2)}) collective-permute-start(f32[16,8,128]{2,1,0:T(8,128)S(1)} %pad_maximum_fusion), channel_id=1, source_target_pairs={{15,31},{16,0},{31,47},{32,16},{47,63},{48,32},{63,79},{64,48},{79... | collective-permute-start | bytes 196616 | tf_op jit(solution)/shard_map/ppermute | solution.py:379
  4.4 21.9 %collective-permute-start.2 = (f32[432,128]{1,0:T(8,128)S(1)}, f32[432,128]{1,0:T(8,128)S(1)}, u32[]{:S(2)}, u32[]{:S(2)}) collective-permute-start(f32[432,128]{1,0:T(8,128)S(1)} %get-tuple-element.30), channel_id=1, source_target_pairs={{0,48},{16,32},{32,16},{48,0},{64,112},{80,96},{96,80},{112,64},{1... | collective-permute-start | bytes 663560 | tf_op jit(solution)/shard_map/ppermute | solution.py:362
  4.9 21.3 %collective-permute-start.3 = (f32[432,128]{1,0:T(8,128)S(1)}, f32[432,128]{1,0:T(8,128)S(1)}, u32[]{:S(2)}, u32[]{:S(2)}) collective-permute-start(f32[432,128]{1,0:T(8,128)S(1)} %get-tuple-element.31), channel_id=1, source_target_pairs={{0,64},{16,80},{32,96},{48,112},{64,0},{80,16},{96,32},{112,48},{1... | collective-permute-start | bytes 663560 | tf_op jit(solution)/shard_map/ppermute | solution.py:362
  7.7 18.6 %collective-permute-start.4 = (f32[432,128]{1,0:T(8,128)S(1)}, f32[432,128]{1,0:T(8,128)S(1)}, u32[]{:S(2)}, u32[]{:S(2)}) collective-permute-start(f32[432,128]{1,0:T(8,128)S(1)} %get-tuple-element.32), channel_id=1, source_target_pairs={{0,80},{16,64},{32,112},{48,96},{64,16},{80,0},{96,48},{112,32},{1... | collective-permute-start | bytes 663560 | tf_op jit(solution)/shard_map/ppermute | solution.py:362
  8.2 18.0 %collective-permute-start.5 = (f32[432,128]{1,0:T(8,128)S(1)}, f32[432,128]{1,0:T(8,128)S(1)}, u32[]{:S(2)}, u32[]{:S(2)}) collective-permute-start(f32[432,128]{1,0:T(8,128)S(1)} %get-tuple-element.33), channel_id=1, source_target_pairs={{0,96},{16,112},{32,64},{48,80},{64,32},{80,48},{96,0},{112,16},{1... | collective-permute-start | bytes 663560 | tf_op jit(solution)/shard_map/ppermute | solution.py:362
  10.7 20.1 %collective-permute-start.6 = (f32[432,128]{1,0:T(8,128)S(1)}, f32[432,128]{1,0:T(8,128)S(1)}, u32[]{:S(2)}, u32[]{:S(2)}) collective-permute-start(f32[432,128]{1,0:T(8,128)S(1)} %get-tuple-element.34), channel_id=1, source_target_pairs={{0,112},{16,96},{32,80},{48,64},{64,48},{80,32},{96,16},{112,0},{1... | collective-permute-start | bytes 663560 | tf_op jit(solution)/shard_map/ppermute | solution.py:362
  14.3 11.9 %all-to-all-start = ((f32[16,16,128]{2,1,0:T(8,128)}), f32[16,16,128]{2,1,0:T(8,128)S(1)}, u32[]{:S(2)}, u32[]{:S(2)}) async-start(f32[16,16,128]{2,1,0:T(8,128)} %concatenate.8), calls=%async_computation | async-start | bytes 262144 | tf_op jit(solution)/shard_map/all_to_all | solution.py:405
  32.5 11.2 %collective-permute-start.8 = (f32[472,128]{1,0:T(8,128)S(1)}, f32[472,128]{1,0:T(8,128)S(1)}, u32[]{:S(2)}, u32[]{:S(2)}) collective-permute-start(f32[472,128]{1,0:T(8,128)S(1)} %get-tuple-element.52), channel_id=1, source_target_pairs={{0,1},{1,0},{2,3},{3,2},{4,5},{5,4},{6,7},{7,6},{8,9},{9,8},{10,11... | collective-permute-start | bytes 725000 | tf_op jit(solution)/shard_map/ppermute | solution.py:370
  37.3 9.2 %collective-permute-start.9 = (f32[472,128]{1,0:T(8,128)S(1)}, f32[472,128]{1,0:T(8,128)S(1)}, u32[]{:S(2)}, u32[]{:S(2)}) collective-permute-start(f32[472,128]{1,0:T(8,128)S(1)} %get-tuple-element.51), channel_id=1, source_target_pairs={{1,2},{2,1},{3,4},{4,3},{5,6},{6,5},{7,8},{8,7},{9,10},{10,9},{11,... | collective-permute-start | bytes 725000 | tf_op jit(solution)/shard_map/ppermute | solution.py:370
  55.0 6.2 %collective-permute-start.10 = (f32[384,128]{1,0:T(8,128)S(1)}, f32[384,128]{1,0:T(8,128)S(1)}, u32[]{:S(2)}, u32[]{:S(2)}) collective-permute-start(f32[384,128]{1,0:T(8,128)S(1)} %get-tuple-element.42), channel_id=1, source_target_pairs={{0,16},{16,0},{32,48},{48,32},{64,80},{80,64},{96,112},{112,96},{1... | collective-permute-start | bytes 589832 | tf_op jit(solution)/shard_map/ppermute | solution.py:362
  56.0 6.5 %collective-permute-start.11 = (f32[384,128]{1,0:T(8,128)S(1)}, f32[384,128]{1,0:T(8,128)S(1)}, u32[]{:S(2)}, u32[]{:S(2)}) collective-permute-start(f32[384,128]{1,0:T(8,128)S(1)} %get-tuple-element.43), channel_id=1, source_target_pairs={{0,32},{16,48},{32,0},{48,16},{64,96},{80,112},{96,64},{112,80},{1... | collective-permute-start | bytes 589832 | tf_op jit(solution)/shard_map/ppermute | solution.py:362
  56.0 11.7 %collective-permute-start.12 = (f32[384,128]{1,0:T(8,128)S(1)}, f32[384,128]{1,0:T(8,128)S(1)}, u32[]{:S(2)}, u32[]{:S(2)}) collective-permute-start(f32[384,128]{1,0:T(8,128)S(1)} %get-tuple-element.44), channel_id=1, source_target_pairs={{0,48},{16,32},{32,16},{48,0},{64,112},{80,96},{96,80},{112,64},{1... | collective-permute-start | bytes 589832 | tf_op jit(solution)/shard_map/ppermute | solution.py:362
  57.8 13.9 %collective-permute-start.13 = (f32[384,128]{1,0:T(8,128)S(1)}, f32[384,128]{1,0:T(8,128)S(1)}, u32[]{:S(2)}, u32[]{:S(2)}) collective-permute-start(f32[384,128]{1,0:T(8,128)S(1)} %get-tuple-element.45), channel_id=1, source_target_pairs={{0,64},{16,80},{32,96},{48,112},{64,0},{80,16},{96,32},{112,48},{1... | collective-permute-start | bytes 589832 | tf_op jit(solution)/shard_map/ppermute | solution.py:362
  58.5 17.8 %collective-permute-start.14 = (f32[384,128]{1,0:T(8,128)S(1)}, f32[384,128]{1,0:T(8,128)S(1)}, u32[]{:S(2)}, u32[]{:S(2)}) collective-permute-start(f32[384,128]{1,0:T(8,128)S(1)} %get-tuple-element.46), channel_id=1, source_target_pairs={{0,80},{16,64},{32,112},{48,96},{64,16},{80,0},{96,48},{112,32},{1... | collective-permute-start | bytes 589832 | tf_op jit(solution)/shard_map/ppermute | solution.py:362
  61.3 16.0 %collective-permute-start.15 = (f32[384,128]{1,0:T(8,128)S(1)}, f32[384,128]{1,0:T(8,128)S(1)}, u32[]{:S(2)}, u32[]{:S(2)}) collective-permute-start(f32[384,128]{1,0:T(8,128)S(1)} %get-tuple-element.47), channel_id=1, source_target_pairs={{0,96},{16,112},{32,64},{48,80},{64,32},{80,48},{96,0},{112,16},{1... | collective-permute-start | bytes 589832 | tf_op jit(solution)/shard_map/ppermute | solution.py:362
  62.5 19.3 %collective-permute-start.16 = (f32[384,128]{1,0:T(8,128)S(1)}, f32[384,128]{1,0:T(8,128)S(1)}, u32[]{:S(2)}, u32[]{:S(2)}) collective-permute-start(f32[384,128]{1,0:T(8,128)S(1)} %get-tuple-element.48), channel_id=1, source_target_pairs={{0,112},{16,96},{32,80},{48,64},{64,48},{80,32},{96,16},{112,0},{1... | collective-permute-start | bytes 589832 | tf_op jit(solution)/shard_map/ppermute | solution.py:362
  81.8 1.1 %copy-start = (f32[3,2,8,2,4,8,128]{6,5,4,3,2,1,0:T(8,128)}, f32[3,2,8,2,4,8,128]{6,5,4,3,2,1,0:T(8,128)S(1)}, u32[]{:S(2)}) copy-start(f32[3,2,8,2,4,8,128]{6,5,4,3,2,1,0:T(8,128)S(1)} %constant_dynamic-update-slice_fusion) | copy-start | bytes 4718596

commit v4 on v3

--- a/solution.py
+++ b/solution.py
@@ -113,7 +113,7 @@
             one(i, c + 1, obs, lambda t: ens_ref[pl.ds(first_row(i, c) + 8 * t, MEMBERS, stride=PITCH), :])
         return carry
 
-    lax.fori_loop(0, COLS, body, 0, unroll=2)
+    lax.fori_loop(0, COLS, body, 0, unroll=16)
     for e, source in enumerate((COLS - 1, 0)):
         obs = obs_ref[source, 8:16, :]
         for i in range(ROWS):
@@ -164,7 +164,7 @@
             put_slab(i * EXT_COLS + c, ref, c * SLAB, source, pair, locs)
         return carry
 
-    lax.fori_loop(0, EXT_COLS, put, 0)
+    lax.fori_loop(0, EXT_COLS, put, 0, unroll=6)
 
     def one(c, carry):
         for i in range(ROWS):
@@ -238,7 +238,7 @@
         put_slab(EXT_COLS + c, below_ref, c * SLAB, source, pair, locs)
         return carry
 
-    lax.fori_loop(0, EXT_COLS, put, 0)
+    lax.fori_loop(0, EXT_COLS, put, 0, unroll=6)
 
     def one_gram(c, carry):
         for i in range(ROWS):
@@ -252,7 +252,7 @@
                 )
         return carry
 
-    lax.fori_loop(0, COLS, one_gram, 0, unroll=8)
+    lax.fori_loop(0, COLS, one_gram, 0, unroll=16)
     member = lax.broadcasted_iota(jnp.int32, (MEMBERS, 128), 0)
     squares = jnp.zeros((MEMBERS, 128), jnp.float32)
     for k in range(MEMBERS):
@@ -325,7 +325,7 @@
                     )
         return carry
 
-    lax.fori_loop(0, COLS, one_update, 0, unroll=8)
+    lax.fori_loop(0, COLS, one_update, 0, unroll=16)
     for s in range(GROUPS):
         for k in range(HELD):
             start = ((m ^ s) * HELD + k) * PITCH

time: 83.2 us -> 81.9 us (0.984)
  Pallas kernels: 15.5 us -> 14 us
    pallas_call x3, Pallas kernels: 14.1 us -> 12.5 us  [vmem_call(): pl.pallas_call(kernel, out_shape=out_shape, in_specs=places, scratch_shap...]
where the time goes in v4:
time: 81.9 us; the launch traced here: 81.6 us
  starting transfers between devices  36.2 us (44%)
  waiting for transfers between devices  28.2 us (34%)
  Pallas kernels  14 us (17%)
  local copies, waits for them, and re-layouts  2.79 us (3%)
    ppermute x14, waiting for transfers between devices, swapped(): return lax.ppermute(x, 'member', [(a, a ^ s) for a in range(GROUPS)])  21.3 us
    ppermute x14, starting transfers between devices, swapped(): return lax.ppermute(x, 'member', [(a, a ^ s) for a in range(GROUPS)])  20.3 us
    pallas_call x3, Pallas kernels, vmem_call(): pl.pallas_call(kernel, out_shape=out_shape, in_specs=places, scratch_shap...  12.5 us
    all_to_all x1, starting transfers between devices, local(): lax.all_to_all(packed, 'region', split_axis=0, concat_axis=0, tiled=True)  8.44 us
    ppermute x2, starting transfers between devices, paired(): return lax.ppermute(x, 'region', pairs)  6.74 us
    all_to_all x1, waiting for transfers between devices, local(): lax.all_to_all(packed, 'region', split_axis=0, concat_axis=0, tiled=True)  3.5 us
    ppermute x2, waiting for transfers between devices, paired(): return lax.ppermute(x, 'region', pairs)  3.46 us
  transfers between devices with their start and end apart: 18, of which 9 were waited for; matrix products, arithmetic and copies ran while one was open for 2% of the time, Pallas kernels for 5%

profile of v4, /device:TPU:113, one launch (start us, length us, event | category | flops | bytes accessed | tf_op | source)
XLA Modules:
  0.0 81.6 jit_solution(16555016759173022196)
XLA Ops:
  0.0 0.0 copy-start.1
  0.0 1.5 %shard_map.58 = (f32[432,128]{1,0:T(8,128)S(1)}, f32[432,128]{1,0:T(8,128)S(1)}, f32[432,128]{1,0:T(8,128)S(1)}, f32[432,128]{1,0:T(8,128)S(1)}, f32[432,128]{1,...) custom-call(s32[1]{0:T(128)} %bitcast.m_ref, f32[3072,128]{1,0:T(8,128)} %bitcast.38), custom_call_target="tpu_custom_call" | custom-call | tf_op jit(solution)/shard_map/pallas_call | solution.py:386
  1.5 0.8 collective-permute-start
  2.2 1.2 %collective-permute-start.1 = (f32[432,128]{1,0:T(8,128)S(1)}, f32[432,128]{1,0:T(8,128)S(1)}, u32[]{:S(2)}, u32[]{:S(2)}) collective-permute-start(f32[432,128]{1,0:T(8,128)S(1)} %get-tuple-element.29), channel_id=1, source_target_pairs={{0,32},{16,48},{32,0},{48,16},{64,96},{80,112},{96,64},{112,80},{1... | collective-permute-start | bytes 663560 | tf_op jit(solution)/shard_map/ppermute | solution.py:362
  3.5 0.0 copy-done.2
  3.5 0.1 fusion.1
  3.7 0.7 collective-permute-start.7
  4.4 0.6 collective-permute-start.2
  4.9 2.7 %collective-permute-start.3 = (f32[432,128]{1,0:T(8,128)S(1)}, f32[432,128]{1,0:T(8,128)S(1)}, u32[]{:S(2)}, u32[]{:S(2)}) collective-permute-start(f32[432,128]{1,0:T(8,128)S(1)} %get-tuple-element.31), channel_id=1, source_target_pairs={{0,64},{16,80},{32,96},{48,112},{64,0},{80,16},{96,32},{112,48},{1... | collective-permute-start | bytes 663560 | tf_op jit(solution)/shard_map/ppermute | solution.py:362
  7.7 0.0 collective-permute-done.7
  7.7 0.5 collective-permute-start.4
  8.2 0.0 collective-permute-done.refs_1_
  8.2 2.5 %collective-permute-start.5 = (f32[432,128]{1,0:T(8,128)S(1)}, f32[432,128]{1,0:T(8,128)S(1)}, u32[]{:S(2)}, u32[]{:S(2)}) collective-permute-start(f32[432,128]{1,0:T(8,128)S(1)} %get-tuple-element.33), channel_id=1, source_target_pairs={{0,96},{16,112},{32,64},{48,80},{64,32},{80,48},{96,0},{112,16},{1... | collective-permute-start | bytes 663560 | tf_op jit(solution)/shard_map/ppermute | solution.py:362
  10.7 0.0 collective-permute-done.1.refs_2_
  10.7 2.3 %collective-permute-start.6 = (f32[432,128]{1,0:T(8,128)S(1)}, f32[432,128]{1,0:T(8,128)S(1)}, u32[]{:S(2)}, u32[]{:S(2)}) collective-permute-start(f32[432,128]{1,0:T(8,128)S(1)} %get-tuple-element.34), channel_id=1, source_target_pairs={{0,112},{16,96},{32,80},{48,64},{64,48},{80,32},{96,16},{112,0},{1... | collective-permute-start | bytes 663560 | tf_op jit(solution)/shard_map/ppermute | solution.py:362
  13.0 1.3 %concatenate.8 = f32[16,16,128]{2,1,0:T(8,128)} concatenate(f32[16,2,128]{2,1,0:T(2,128)S(1)} %bitcast.51, f32[16,2,128]{2,1,0:T(2,128)S(1)} %bitcast.47, f32[16,2,128]{2,1,0:T(2,128)S(1)} %bitcast.49, f32[16,2,128]{2,1,0:T(2,128)S(1)} %reshape.93, f32[16,8,128]{2,1,0:T(8,128)S(1)} %collective-permute-done.7), dimensions={1} | concatenate | bytes 262144 | tf_op jit(solution)/shard_map/concatenate | solution.py:402
  14.3 8.4 %all-to-all-start = ((f32[16,16,128]{2,1,0:T(8,128)}), f32[16,16,128]{2,1,0:T(8,128)S(1)}, u32[]{:S(2)}, u32[]{:S(2)}) async-start(f32[16,16,128]{2,1,0:T(8,128)} %concatenate.8), calls=%async_computation | async-start | bytes 262144 | tf_op jit(solution)/shard_map/all_to_all | solution.py:405
  22.8 3.5 %all-to-all-done.refs_8_ = f32[16,16,128]{2,1,0:T(8,128)S(1)} async-done(((f32[16,16,128]{2,1,0:T(8,128)}), f32[16,16,128]{2,1,0:T(8,128)S(1)}, u32[]{:S(2)}, u32[]{:S(2)}) %all-to-all-start) | async-done | bytes 131104 | tf_op jit(solution)/shard_map/all_to_all | solution.py:405
  26.3 0.0 collective-permute-done.2.refs_3_
  26.3 0.0 collective-permute-done.3.refs_4_
  26.3 0.0 collective-permute-done.4.refs_5_
  26.3 0.0 collective-permute-done.5.refs_6_
  26.3 4.5 %collective-permute-done.6.refs_7_ = f32[432,128]{1,0:T(8,128)S(1)} collective-permute-done((f32[432,128]{1,0:T(8,128)S(1)}, f32[432,128]{1,0:T(8,128)S(1)}, u32[]{:S(2)}, u32[]{:S(2)}) %collective-permute-start.6) | collective-permute-done | bytes 221216 | tf_op jit(solution)/shard_map/ppermute | solution.py:362
  30.8 0.8 shard_map.59
  31.6 0.1 broadcast_select_fusion.2
  31.6 4.8 %collective-permute-start.8 = (f32[472,128]{1,0:T(8,128)S(1)}, f32[472,128]{1,0:T(8,128)S(1)}, u32[]{:S(2)}, u32[]{:S(2)}) collective-permute-start(f32[472,128]{1,0:T(8,128)S(1)} %get-tuple-element.52), channel_id=1, source_target_pairs={{0,1},{1,0},{2,3},{3,2},{4,5},{5,4},{6,7},{7,6},{8,9},{9,8},{10,11... | collective-permute-start | bytes 725000 | tf_op jit(solution)/shard_map/ppermute | solution.py:370
  36.5 1.9 %collective-permute-start.9 = (f32[472,128]{1,0:T(8,128)S(1)}, f32[472,128]{1,0:T(8,128)S(1)}, u32[]{:S(2)}, u32[]{:S(2)}) collective-permute-start(f32[472,128]{1,0:T(8,128)S(1)} %get-tuple-element.51), channel_id=1, source_target_pairs={{1,2},{2,1},{3,4},{4,3},{5,6},{6,5},{7,8},{8,7},{9,10},{10,9},{11,... | collective-permute-start | bytes 725000 | tf_op jit(solution)/shard_map/ppermute | solution.py:370
  38.4 3.8 %shard_map.60 = (f32[3584,128]{1,0:T(8,128)S(1)}, bf16[64,80,256]{2,1,0:T(8,128)(2,1)S(1)}, f32[128,128]{1,0:T(8,128)S(1)}) custom-call(f32[472,128]{1,0:T(8,128)S(1)} %get-tuple-element.35.slab0_ref, f32[472,128]{1,0:T(8,128)S(1)} %get-tuple-element.36.slab1_ref, f32[3168,128]{1,0:T(8,128)S(1)} %get-tuple-element.37.ens_ref), custom_call_target="tpu_custom_call" | custom-call | flops 4000000000 | tf_op jit(solution)/shard_map/pallas_call | solution.py:351
  42.2 0.6 collective-permute-done.8
  42.9 2.8 %collective-permute-done.9 = f32[472,128]{1,0:T(8,128)S(1)} collective-permute-done((f32[472,128]{1,0:T(8,128)S(1)}, f32[472,128]{1,0:T(8,128)S(1)}, u32[]{:S(2)}, u32[]{:S(2)}) %collective-permute-start.9) | collective-permute-done | bytes 241696 | tf_op jit(solution)/shard_map/ppermute | solution.py:370
  45.7 7.9 %shard_map.61 = (f32[384,128]{1,0:T(8,128)S(1)}, f32[384,128]{1,0:T(8,128)S(1)}, f32[384,128]{1,0:T(8,128)S(1)}, f32[384,128]{1,0:T(8,128)S(1)}, f32[384,128]{1,...) custom-call(s32[1]{0:T(128)} %bitcast.m_ref, ...), custom_call_target="tpu_custom_call" | custom-call | flops 10000000000 | tf_op jit(solution)/shard_map/pallas_call | solution.py:351
  53.7 1.0 %collective-permute-start.10 = (f32[384,128]{1,0:T(8,128)S(1)}, f32[384,128]{1,0:T(8,128)S(1)}, u32[]{:S(2)}, u32[]{:S(2)}) collective-permute-start(f32[384,128]{1,0:T(8,128)S(1)} %get-tuple-element.42), channel_id=1, source_target_pairs={{0,16},{16,0},{32,48},{48,32},{64,80},{80,64},{96,112},{112,96},{1... | collective-permute-start | bytes 589832 | tf_op jit(solution)/shard_map/ppermute | solution.py:362
  54.7 0.0 collective-permute-start.11
  54.7 1.8 %collective-permute-start.12 = (f32[384,128]{1,0:T(8,128)S(1)}, f32[384,128]{1,0:T(8,128)S(1)}, u32[]{:S(2)}, u32[]{:S(2)}) collective-permute-start(f32[384,128]{1,0:T(8,128)S(1)} %get-tuple-element.44), channel_id=1, source_target_pairs={{0,48},{16,32},{32,16},{48,0},{64,112},{80,96},{96,80},{112,64},{1... | collective-permute-start | bytes 589832 | tf_op jit(solution)/shard_map/ppermute | solution.py:362
  56.4 0.7 collective-permute-start.13
  57.2 2.5 %collective-permute-start.14 = (f32[384,128]{1,0:T(8,128)S(1)}, f32[384,128]{1,0:T(8,128)S(1)}, u32[]{:S(2)}, u32[]{:S(2)}) collective-permute-start(f32[384,128]{1,0:T(8,128)S(1)} %get-tuple-element.46), channel_id=1, source_target_pairs={{0,80},{16,64},{32,112},{48,96},{64,16},{80,0},{96,48},{112,32},{1... | collective-permute-start | bytes 589832 | tf_op jit(solution)/shard_map/ppermute | solution.py:362
  59.7 0.2 broadcast_in_dim.12
  59.9 0.0 collective-permute-done.10
  59.9 1.3 %collective-permute-start.15 = (f32[384,128]{1,0:T(8,128)S(1)}, f32[384,128]{1,0:T(8,128)S(1)}, u32[]{:S(2)}, u32[]{:S(2)}) collective-permute-start(f32[384,128]{1,0:T(8,128)S(1)} %get-tuple-element.47), channel_id=1, source_target_pairs={{0,96},{16,112},{32,64},{48,80},{64,32},{80,48},{96,0},{112,16},{1... | collective-permute-start | bytes 589832 | tf_op jit(solution)/shard_map/ppermute | solution.py:362
  61.2 0.0 collective-permute-done.11
  61.2 2.5 %collective-permute-start.16 = (f32[384,128]{1,0:T(8,128)S(1)}, f32[384,128]{1,0:T(8,128)S(1)}, u32[]{:S(2)}, u32[]{:S(2)}) collective-permute-start(f32[384,128]{1,0:T(8,128)S(1)} %get-tuple-element.48), channel_id=1, source_target_pairs={{0,112},{16,96},{32,80},{48,64},{64,48},{80,32},{96,16},{112,0},{1... | collective-permute-start | bytes 589832 | tf_op jit(solution)/shard_map/ppermute | solution.py:362
  63.7 2.7 %collective-permute-done.12 = f32[384,128]{1,0:T(8,128)S(1)} collective-permute-done((f32[384,128]{1,0:T(8,128)S(1)}, f32[384,128]{1,0:T(8,128)S(1)}, u32[]{:S(2)}, u32[]{:S(2)}) %collective-permute-start.12) | collective-permute-done | bytes 196640 | tf_op jit(solution)/shard_map/ppermute | solution.py:362
  66.4 3.9 %collective-permute-done.13 = f32[384,128]{1,0:T(8,128)S(1)} collective-permute-done((f32[384,128]{1,0:T(8,128)S(1)}, f32[384,128]{1,0:T(8,128)S(1)}, u32[]{:S(2)}, u32[]{:S(2)}) %collective-permute-start.13) | collective-permute-done | bytes 196640 | tf_op jit(solution)/shard_map/ppermute | solution.py:362
  70.4 4.6 %collective-permute-done.14 = f32[384,128]{1,0:T(8,128)S(1)} collective-permute-done((f32[384,128]{1,0:T(8,128)S(1)}, f32[384,128]{1,0:T(8,128)S(1)}, u32[]{:S(2)}, u32[]{:S(2)}) %collective-permute-start.14) | collective-permute-done | bytes 196640 | tf_op jit(solution)/shard_map/ppermute | solution.py:362
  75.0 1.0 %collective-permute-done.15 = f32[384,128]{1,0:T(8,128)S(1)} collective-permute-done((f32[384,128]{1,0:T(8,128)S(1)}, f32[384,128]{1,0:T(8,128)S(1)}, u32[]{:S(2)}, u32[]{:S(2)}) %collective-permute-start.15) | collective-permute-done | bytes 196640 | tf_op jit(solution)/shard_map/ppermute | solution.py:362
  76.0 4.5 %collective-permute-done.16 = f32[384,128]{1,0:T(8,128)S(1)} collective-permute-done((f32[384,128]{1,0:T(8,128)S(1)}, f32[384,128]{1,0:T(8,128)S(1)}, u32[]{:S(2)}, u32[]{:S(2)}) %collective-permute-start.16) | collective-permute-done | bytes 196640 | tf_op jit(solution)/shard_map/ppermute | solution.py:362
  80.5 0.0 copy-start
  80.5 1.1 %copy-done = f32[3,2,8,2,4,8,128]{6,5,4,3,2,1,0:T(8,128)} copy-done((f32[3,2,8,2,4,8,128]{6,5,4,3,2,1,0:T(8,128)}, f32[3,2,8,2,4,8,128]{6,5,4,3,2,1,0:T(8,128)S(1)}, u32[]{:S(2)}) %copy-start) | copy-done | bytes 1572888
  (18 shorter events, 0.2 us)
Async XLA Ops:
  0.0 3.5 %copy-start.4 = (s32[32,1]{0,1:T(1,128)S(1)}, s32[32,1]{0,1:T(1,128)}, u32[]{:S(2)}) copy-start(s32[32,1]{0,1:T(1,128)} %param.9) | copy-start | bytes 388
  0.0 3.5 %copy-start.2 = (f32[32,1,128]{2,1,0:T(1,128)S(1)}, f32[32,1,128]{2,1,0:T(1,128)}, u32[]{:S(2)}) copy-start(f32[32,1,128]{2,1,0:T(1,128)} %param.7) | copy-start | bytes 49156
  0.0 3.6 %copy-start.3 = (s32[32,1,128]{2,1,0:T(1,128)S(1)}, s32[32,1,128]{2,1,0:T(1,128)}, u32[]{:S(2)}) copy-start(s32[32,1,128]{2,1,0:T(1,128)} %param.8) | copy-start | bytes 49156
  0.0 3.6 %copy-start.1 = (f32[32,1,128]{2,1,0:T(1,128)S(1)}, f32[32,1,128]{2,1,0:T(1,128)}, u32[]{:S(2)}) copy-start(f32[32,1,128]{2,1,0:T(1,128)} %param.6) | copy-start | bytes 49156
  1.5 6.7 %collective-permute-start = (f32[432,128]{1,0:T(8,128)S(1)}, f32[432,128]{1,0:T(8,128)S(1)}, u32[]{:S(2)}, u32[]{:S(2)}) collective-permute-start(f32[432,128]{1,0:T(8,128)S(1)} %get-tuple-element.28), channel_id=1, source_target_pairs={{0,16},{16,0},{32,48},{48,32},{64,80},{80,64},{96,112},{112,96},{1... | collective-permute-start | bytes 663560 | tf_op jit(solution)/shard_map/ppermute | solution.py:362
  2.2 8.5 %collective-permute-start.1 = (f32[432,128]{1,0:T(8,128)S(1)}, f32[432,128]{1,0:T(8,128)S(1)}, u32[]{:S(2)}, u32[]{:S(2)}) collective-permute-start(f32[432,128]{1,0:T(8,128)S(1)} %get-tuple-element.29), channel_id=1, source_target_pairs={{0,32},{16,48},{32,0},{48,16},{64,96},{80,112},{96,64},{112,80},{1... | collective-permute-start | bytes 663560 | tf_op jit(solution)/shard_map/ppermute | solution.py:362
  3.7 4.0 %collective-permute-start.7 = (f32[16,8,128]{2,1,0:T(8,128)S(1)}, f32[16,8,128]{2,1,0:T(8,128)S(1)}, u32[]{:S(2)}, u32[]{:S(2)}) collective-permute-start(f32[16,8,128]{2,1,0:T(8,128)S(1)} %pad_maximum_fusion), channel_id=1, source_target_pairs={{15,31},{16,0},{31,47},{32,16},{47,63},{48,32},{63,79},{64,48},{79... | collective-permute-start | bytes 196616 | tf_op jit(solution)/shard_map/ppermute | solution.py:379
  4.4 21.9 %collective-permute-start.2 = (f32[432,128]{1,0:T(8,128)S(1)}, f32[432,128]{1,0:T(8,128)S(1)}, u32[]{:S(2)}, u32[]{:S(2)}) collective-permute-start(f32[432,128]{1,0:T(8,128)S(1)} %get-tuple-element.30), channel_id=1, source_target_pairs={{0,48},{16,32},{32,16},{48,0},{64,112},{80,96},{96,80},{112,64},{1... | collective-permute-start | bytes 663560 | tf_op jit(solution)/shard_map/ppermute | solution.py:362
  4.9 21.3 %collective-permute-start.3 = (f32[432,128]{1,0:T(8,128)S(1)}, f32[432,128]{1,0:T(8,128)S(1)}, u32[]{:S(2)}, u32[]{:S(2)}) collective-permute-start(f32[432,128]{1,0:T(8,128)S(1)} %get-tuple-element.31), channel_id=1, source_target_pairs={{0,64},{16,80},{32,96},{48,112},{64,0},{80,16},{96,32},{112,48},{1... | collective-permute-start | bytes 663560 | tf_op jit(solution)/shard_map/ppermute | solution.py:362
  7.7 18.6 %collective-permute-start.4 = (f32[432,128]{1,0:T(8,128)S(1)}, f32[432,128]{1,0:T(8,128)S(1)}, u32[]{:S(2)}, u32[]{:S(2)}) collective-permute-start(f32[432,128]{1,0:T(8,128)S(1)} %get-tuple-element.32), channel_id=1, source_target_pairs={{0,80},{16,64},{32,112},{48,96},{64,16},{80,0},{96,48},{112,32},{1... | collective-permute-start | bytes 663560 | tf_op jit(solution)/shard_map/ppermute | solution.py:362
  8.2 18.0 %collective-permute-start.5 = (f32[432,128]{1,0:T(8,128)S(1)}, f32[432,128]{1,0:T(8,128)S(1)}, u32[]{:S(2)}, u32[]{:S(2)}) collective-permute-start(f32[432,128]{1,0:T(8,128)S(1)} %get-tuple-element.33), channel_id=1, source_target_pairs={{0,96},{16,112},{32,64},{48,80},{64,32},{80,48},{96,0},{112,16},{1... | collective-permute-start | bytes 663560 | tf_op jit(solution)/shard_map/ppermute | solution.py:362
  10.7 20.1 %collective-permute-start.6 = (f32[432,128]{1,0:T(8,128)S(1)}, f32[432,128]{1,0:T(8,128)S(1)}, u32[]{:S(2)}, u32[]{:S(2)}) collective-permute-start(f32[432,128]{1,0:T(8,128)S(1)} %get-tuple-element.34), channel_id=1, source_target_pairs={{0,112},{16,96},{32,80},{48,64},{64,48},{80,32},{96,16},{112,0},{1... | collective-permute-start | bytes 663560 | tf_op jit(solution)/shard_map/ppermute | solution.py:362
  14.3 11.9 %all-to-all-start = ((f32[16,16,128]{2,1,0:T(8,128)}), f32[16,16,128]{2,1,0:T(8,128)S(1)}, u32[]{:S(2)}, u32[]{:S(2)}) async-start(f32[16,16,128]{2,1,0:T(8,128)} %concatenate.8), calls=%async_computation | async-start | bytes 262144 | tf_op jit(solution)/shard_map/all_to_all | solution.py:405
  31.6 11.2 %collective-permute-start.8 = (f32[472,128]{1,0:T(8,128)S(1)}, f32[472,128]{1,0:T(8,128)S(1)}, u32[]{:S(2)}, u32[]{:S(2)}) collective-permute-start(f32[472,128]{1,0:T(8,128)S(1)} %get-tuple-element.52), channel_id=1, source_target_pairs={{0,1},{1,0},{2,3},{3,2},{4,5},{5,4},{6,7},{7,6},{8,9},{9,8},{10,11... | collective-permute-start | bytes 725000 | tf_op jit(solution)/shard_map/ppermute | solution.py:370
  36.5 9.2 %collective-permute-start.9 = (f32[472,128]{1,0:T(8,128)S(1)}, f32[472,128]{1,0:T(8,128)S(1)}, u32[]{:S(2)}, u32[]{:S(2)}) collective-permute-start(f32[472,128]{1,0:T(8,128)S(1)} %get-tuple-element.51), channel_id=1, source_target_pairs={{1,2},{2,1},{3,4},{4,3},{5,6},{6,5},{7,8},{8,7},{9,10},{10,9},{11,... | collective-permute-start | bytes 725000 | tf_op jit(solution)/shard_map/ppermute | solution.py:370
  53.7 6.2 %collective-permute-start.10 = (f32[384,128]{1,0:T(8,128)S(1)}, f32[384,128]{1,0:T(8,128)S(1)}, u32[]{:S(2)}, u32[]{:S(2)}) collective-permute-start(f32[384,128]{1,0:T(8,128)S(1)} %get-tuple-element.42), channel_id=1, source_target_pairs={{0,16},{16,0},{32,48},{48,32},{64,80},{80,64},{96,112},{112,96},{1... | collective-permute-start | bytes 589832 | tf_op jit(solution)/shard_map/ppermute | solution.py:362
  54.7 6.5 %collective-permute-start.11 = (f32[384,128]{1,0:T(8,128)S(1)}, f32[384,128]{1,0:T(8,128)S(1)}, u32[]{:S(2)}, u32[]{:S(2)}) collective-permute-start(f32[384,128]{1,0:T(8,128)S(1)} %get-tuple-element.43), channel_id=1, source_target_pairs={{0,32},{16,48},{32,0},{48,16},{64,96},{80,112},{96,64},{112,80},{1... | collective-permute-start | bytes 589832 | tf_op jit(solution)/shard_map/ppermute | solution.py:362
  54.7 11.7 %collective-permute-start.12 = (f32[384,128]{1,0:T(8,128)S(1)}, f32[384,128]{1,0:T(8,128)S(1)}, u32[]{:S(2)}, u32[]{:S(2)}) collective-permute-start(f32[384,128]{1,0:T(8,128)S(1)} %get-tuple-element.44), channel_id=1, source_target_pairs={{0,48},{16,32},{32,16},{48,0},{64,112},{80,96},{96,80},{112,64},{1... | collective-permute-start | bytes 589832 | tf_op jit(solution)/shard_map/ppermute | solution.py:362
  56.4 13.9 %collective-permute-start.13 = (f32[384,128]{1,0:T(8,128)S(1)}, f32[384,128]{1,0:T(8,128)S(1)}, u32[]{:S(2)}, u32[]{:S(2)}) collective-permute-start(f32[384,128]{1,0:T(8,128)S(1)} %get-tuple-element.45), channel_id=1, source_target_pairs={{0,64},{16,80},{32,96},{48,112},{64,0},{80,16},{96,32},{112,48},{1... | collective-permute-start | bytes 589832 | tf_op jit(solution)/shard_map/ppermute | solution.py:362
  57.2 17.8 %collective-permute-start.14 = (f32[384,128]{1,0:T(8,128)S(1)}, f32[384,128]{1,0:T(8,128)S(1)}, u32[]{:S(2)}, u32[]{:S(2)}) collective-permute-start(f32[384,128]{1,0:T(8,128)S(1)} %get-tuple-element.46), channel_id=1, source_target_pairs={{0,80},{16,64},{32,112},{48,96},{64,16},{80,0},{96,48},{112,32},{1... | collective-permute-start | bytes 589832 | tf_op jit(solution)/shard_map/ppermute | solution.py:362
  59.9 16.0 %collective-permute-start.15 = (f32[384,128]{1,0:T(8,128)S(1)}, f32[384,128]{1,0:T(8,128)S(1)}, u32[]{:S(2)}, u32[]{:S(2)}) collective-permute-start(f32[384,128]{1,0:T(8,128)S(1)} %get-tuple-element.47), channel_id=1, source_target_pairs={{0,96},{16,112},{32,64},{48,80},{64,32},{80,48},{96,0},{112,16},{1... | collective-permute-start | bytes 589832 | tf_op jit(solution)/shard_map/ppermute | solution.py:362
  61.2 19.3 %collective-permute-start.16 = (f32[384,128]{1,0:T(8,128)S(1)}, f32[384,128]{1,0:T(8,128)S(1)}, u32[]{:S(2)}, u32[]{:S(2)}) collective-permute-start(f32[384,128]{1,0:T(8,128)S(1)} %get-tuple-element.48), channel_id=1, source_target_pairs={{0,112},{16,96},{32,80},{48,64},{64,48},{80,32},{96,16},{112,0},{1... | collective-permute-start | bytes 589832 | tf_op jit(solution)/shard_map/ppermute | solution.py:362
  80.5 1.1 %copy-start = (f32[3,2,8,2,4,8,128]{6,5,4,3,2,1,0:T(8,128)}, f32[3,2,8,2,4,8,128]{6,5,4,3,2,1,0:T(8,128)S(1)}, u32[]{:S(2)}) copy-start(f32[3,2,8,2,4,8,128]{6,5,4,3,2,1,0:T(8,128)S(1)} %constant_dynamic-update-slice_fusion) | copy-start | bytes 4718596
